TPU v7x, 8 devices: a whole 2x2x1 slice. The times are simulated.
8 devices in a mesh: batch: 1 (over z), z: 2 (over y), y: 2 (over x), x: 2 (over core).
Axes of the slice: x: 2, y: 2, z: 1, core: 2. Of those that a mesh axis runs over, the one named last changes fastest.
Arguments:
- source: float32 [192, 192, 192], P(('batch', 'z'), 'y', 'x')
- initial_guess: float32 [192, 192, 192], P(('batch', 'z'), 'y', 'x')
Outputs:
- output: float32 [192, 192, 192], P(('batch', 'z'), 'y', 'x')
All inputs are finite; a program needn't handle non-finite values.
Results may differ from a plain program's by a relative error of at most 0.001.
Values sent between devices are 32-bit elements.
A program may use at most 1 GiB of HBM per device.

v0:
```python
import jax
import jax.numpy as jnp
from jax import lax
from jax.sharding import PartitionSpec as P

CYCLES = 2
PRE = 2
POST = 2
COARSE_SWEEPS = 24
GRID_AXES = ('z', 'y', 'x')


def level_count(fine_edge):
    count = 0
    edge_now = fine_edge
    for step_index in range(16):
        if edge_now % 2 == 0 and edge_now // 2 >= 4:
            edge_now = edge_now // 2
            count = count + 1
    return count


def split_level(fine_edge, levels, counts):
    deepest = 0
    for level in range(1, levels + 1):
        if deepest == level - 1 and all((fine_edge >> level) % count == 0 for count in counts):
            deepest = level
    return deepest


def halo_planes(grid, axis, count):
    extent = grid.shape[axis]
    first = lax.slice_in_dim(grid, 0, 1, axis=axis)
    last = lax.slice_in_dim(grid, extent - 1, extent, axis=axis)
    if count == 1:
        return -first, -last
    axis_name = GRID_AXES[axis]
    position = lax.axis_index(axis_name)
    upward = [(rank_id, rank_id + 1) for rank_id in range(count - 1)]
    downward = [(rank_id + 1, rank_id) for rank_id in range(count - 1)]
    from_below = lax.ppermute(last, axis_name, upward)
    from_above = lax.ppermute(first, axis_name, downward)
    lower = jnp.where(position == 0, -first, from_below)
    upper = jnp.where(position == count - 1, -last, from_above)
    return lower, upper


def shifted(grid, axis, count):
    lower, upper = halo_planes(grid, axis, count)
    extent = grid.shape[axis]
    below = jnp.concatenate([lower, lax.slice_in_dim(grid, 0, extent - 1, axis=axis)], axis=axis)
    above = jnp.concatenate([lax.slice_in_dim(grid, 1, extent, axis=axis), upper], axis=axis)
    return below, above


def neighbour_sum(grid, grid_counts):
    total = jnp.zeros_like(grid)
    for axis in range(3):
        below, above = shifted(grid, axis, grid_counts[axis])
        total = total + below + above
    return total


def red_mask(local_shape, grid_counts):
    parity = 0
    for axis in range(3):
        coords = jnp.arange(local_shape[axis], dtype=jnp.int32)
        if grid_counts[axis] > 1:
            coords = coords + lax.axis_index(GRID_AXES[axis]) * local_shape[axis]
        bcast_shape = [1, 1, 1]
        bcast_shape[axis] = local_shape[axis]
        parity = parity + coords.reshape(bcast_shape)
    return parity % 2 == 0


def gs_sweep(iterate, source, step_sq, red_cells, grid_counts):
    scaled = step_sq * source
    updated = (scaled + neighbour_sum(iterate, grid_counts)) / 6.0
    iterate = jnp.where(red_cells, updated, iterate)
    updated = (scaled + neighbour_sum(iterate, grid_counts)) / 6.0
    return jnp.where(red_cells, iterate, updated)


def residual(iterate, source, step_sq, grid_counts):
    return source - (6.0 * iterate - neighbour_sum(iterate, grid_counts)) / step_sq


def restrict(grid):
    grid_shape = grid.shape
    folded = grid.reshape(grid_shape[0] // 2, 2, grid_shape[1] // 2, 2, grid_shape[2] // 2, 2)
    return folded.mean(axis=(1, 3, 5))


def prolong(coarse, grid_counts):
    fine = coarse
    for axis in range(3):
        below, above = shifted(fine, axis, grid_counts[axis])
        even_cells = 0.75 * fine + 0.25 * below
        odd_cells = 0.75 * fine + 0.25 * above
        new_shape = list(fine.shape)
        new_shape[axis] = 2 * new_shape[axis]
        fine = jnp.stack([even_cells, odd_cells], axis=axis + 1).reshape(new_shape)
    return fine


def gather_grid(block, grid_counts):
    whole = block
    for axis in range(3):
        if grid_counts[axis] > 1:
            whole = lax.all_gather(whole, GRID_AXES[axis], axis=axis, tiled=True)
    return whole


def own_block(whole, local_shape, grid_counts):
    starts = []
    for axis in range(3):
        if grid_counts[axis] > 1:
            starts.append(lax.axis_index(GRID_AXES[axis]) * local_shape[axis])
        else:
            starts.append(0)
    return lax.dynamic_slice(whole, starts, local_shape)


def vcycle(iterate, source, level, fine_edge, levels, deepest, grid_counts):
    step_sq = (1.0 / (fine_edge >> level)) ** 2
    red_cells = red_mask(iterate.shape, grid_counts)
    if level == levels:
        return lax.fori_loop(0, COARSE_SWEEPS, lambda sweep_index, current: gs_sweep(current, source, step_sq, red_cells, grid_counts), iterate)
    for sweep_index in range(PRE):
        iterate = gs_sweep(iterate, source, step_sq, red_cells, grid_counts)
    residue = residual(iterate, source, step_sq, grid_counts)
    if level < deepest:
        coarse_source = restrict(residue)
        coarse_sol = vcycle(jnp.zeros_like(coarse_source), coarse_source, level + 1, fine_edge, levels, deepest, grid_counts)
        correction = prolong(coarse_sol, grid_counts)
    else:
        single = (1, 1, 1)
        coarse_source = restrict(gather_grid(residue, grid_counts))
        coarse_sol = vcycle(jnp.zeros_like(coarse_source), coarse_source, level + 1, fine_edge, levels, levels, single)
        correction = own_block(prolong(coarse_sol, single), residue.shape, grid_counts)
    iterate = iterate + correction
    for sweep_index in range(POST):
        iterate = gs_sweep(iterate, source, step_sq, red_cells, grid_counts)
    return iterate


def solution(mesh):
    counts = tuple(mesh.shape[axis_name] for axis_name in GRID_AXES)
    grid_spec = P(('batch', 'z'), 'y', 'x')

    def local_solve(source, initial_guess):
        fine_edge = source.shape[0] * counts[0]
        levels = level_count(fine_edge)
        deepest = split_level(fine_edge, levels, counts)
        iterate = initial_guess
        for cycle_index in range(CYCLES):
            iterate = vcycle(iterate, source, 0, fine_edge, levels, deepest, counts)
        return iterate

    return jax.shard_map(local_solve, mesh=mesh, in_specs=(grid_spec, grid_spec), out_specs=grid_spec, check_vma=False)
```

profile of v0, /device:TPU:0, one launch (start us, length us, event | category | flops | bytes accessed | tf_op | source)
XLA Modules:
  0.0 5490.3 jit_solution(5538485919281807552)
XLA Ops:
  8.7 7.3 copy.1654
  16.0 8.8 fusion.831
  26.9 8.8 fusion.828
  52.6 7.3 copy.1653
  153.6 10.2 negate_select_fusion.53
  165.9 17.2 fusion.44
  233.3 10.2 negate_select_fusion.51
  245.7 17.2 fusion.51
  312.0 10.2 negate_select_fusion.49
  324.4 17.2 fusion.58
  391.0 10.2 negate_select_fusion.47
  403.3 17.2 fusion.65
  469.8 10.1 negate_select_fusion.45
  482.1 18.9 fusion.72
  501.0 7.4 copy.1688
  508.4 130.7 %reshape.2020 = f32[48,2,48,2,48,2]{5,4,3,2,1,0:T(8,128)} reshape(f32[96,96,96]{2,1,0:T(8,128)} %copy.1688) | data formatting | bytes 7077888 | tf_op jit(solution)/shard_map/reshape | solution.py:90
  639.0 68.1 %reduce_sum.90 = f32[48,48,48]{2,1,0:T(8,128)S(1)} reduce(f32[48,2,48,2,48,2]{5,4,3,2,1,0:T(8,128)} %reshape.2020, f32[]{:T(128)} %constant.342.clone.1), dimensions={1,3,5}, to_apply=%region_0.1 | reduce | flops 774144 | bytes 3981316 | tf_op jit(solution)/shard_map/reduce_sum | solution.py:91
  866.0 13.6 reshape.2021
  879.6 10.3 reduce_sum.91
  1101.2 845.2 %while.22 = (s32[]{:T(128)}, f32[3,3,3]{2,1,0:T(4,128)S(1)}, f32[3,3,3]{2,1,0:T(4,128)S(1)}, s32[3]{0:T(128)S(1)}, s32[3,3]{1,0:T(4,128)S(1)}, /*index=5*/s32[]{:T(128)}, s32[]{:T(128)}, u32[]{:T(128)}, u32[]{:T(128)}) while((s32[]{:T(128)}, f32[3,3,3]{2,1,0:T(4,128)S(1)}, f32[3,3,3]{2,1,0:T(4,128)S(1)}, s32[3]{0:T(128)S(1)}, ...), condition=%wide.region_6.7_spmd.clone, body=%wide.region_5.6_spmd.clone.sunk | while | flops 1799 | bytes 8606 | solution.py:128
  2233.5 5.7 collective-permute-start.266
  2440.4 6.3 collective-permute-start.296
  2466.3 6.6 copy.1801
  2472.9 6.0 copy.1802
  2527.0 10.2 negate_select_fusion.43
  2539.4 17.2 fusion.79
  2605.9 10.2 negate_select_fusion.41
  2618.3 17.2 fusion.86
  2684.9 10.2 negate_select_fusion.39
  2697.2 17.2 fusion.93
  2763.6 10.2 negate_select_fusion.37
  2775.9 17.2 fusion.100
  2842.5 10.2 negate_select_fusion.35
  2854.9 17.2 fusion.107
  2921.3 10.2 negate_select_fusion.33
  2933.6 17.2 fusion.114
  3000.2 10.2 negate_select_fusion.31
  3012.6 17.2 fusion.121
  3078.9 10.2 negate_select_fusion.29
  3091.3 17.2 fusion.128
  3158.0 10.1 negate_select_fusion.27
  3170.2 18.9 fusion.135
  3189.2 7.4 copy.1840
  3196.5 130.7 %reshape.2040 = f32[48,2,48,2,48,2]{5,4,3,2,1,0:T(8,128)} reshape(f32[96,96,96]{2,1,0:T(8,128)} %copy.1840) | data formatting | bytes 7077888 | tf_op jit(solution)/shard_map/reshape | solution.py:90
  3327.2 68.1 %reduce_sum.95 = f32[48,48,48]{2,1,0:T(8,128)S(1)} reduce(f32[48,2,48,2,48,2]{5,4,3,2,1,0:T(8,128)} %reshape.2040, f32[]{:T(128)} %constant.342.clone.1), dimensions={1,3,5}, to_apply=%region_7.8 | reduce | flops 774144 | bytes 3981316 | tf_op jit(solution)/shard_map/reduce_sum | solution.py:91
  3500.4 5.5 collective-permute-start.366
  3538.3 5.5 collective-permute-start.372
  3554.0 13.6 reshape.2041
  3567.6 10.3 reduce_sum.96
  3789.1 845.2 %while.23 = (s32[]{:T(128)}, f32[3,3,3]{2,1,0:T(4,128)S(1)}, f32[3,3,3]{2,1,0:T(4,128)S(1)}, s32[3]{0:T(128)S(1)}, s32[3,3]{1,0:T(4,128)S(1)}, /*index=5*/s32[]{:T(128)}, s32[]{:T(128)}, u32[]{:T(128)}, u32[]{:T(128)}) while((s32[]{:T(128)}, f32[3,3,3]{2,1,0:T(4,128)S(1)}, f32[3,3,3]{2,1,0:T(4,128)S(1)}, s32[3]{0:T(128)S(1)}, ...), condition=%wide.region_13.14_spmd.clone, body=%wide.region_12.13_spmd.clone.sunk | while | flops 1799 | bytes 8606 | solution.py:128
  4921.4 5.7 collective-permute-start.542
  5055.5 5.5 collective-permute-start.558
  5128.2 6.3 collective-permute-start.572
  5154.1 6.6 copy.1954
  5160.7 6.0 copy.1955
  5214.6 10.2 negate_select_fusion.25
  5226.9 17.2 fusion.142
  5293.7 10.2 negate_select_fusion.23
  5306.0 17.2 fusion.149
  5372.4 10.2 negate_select_fusion.21
  5384.7 17.2 fusion.156
  5451.1 10.2 negate_select_fusion.19
  5463.4 19.3 fusion.163
  5482.7 7.3 copy.1972
  (5032 shorter events, 4401.3 us)
Async XLA Ops:
  0.0 129.0 %collective-permute-start.59 = (f32[48,48,1]{1,0,2:T(8,128)S(1)}, f32[48,48,1]{1,0,2:T(8,128)S(1)}, u32[]{:S(2)}, u32[]{:S(2)}) collective-permute-start(f32[48,48,1]{1,0,2:T(8,128)S(1)} %broadcast.1211), channel_id=1, source_target_pairs={{1,0},{3,2},{5,4},{7,6}} | collective-permute-start | bytes 27656 | tf_op jit(solution)/shard_map/ppermute | solution.py:42
  1.3 134.0 %collective-permute-start.58 = (f32[48,48,1]{1,0,2:T(8,128)S(1)}, f32[48,48,1]{1,0,2:T(8,128)S(1)}, u32[]{:S(2)}, u32[]{:S(2)}) collective-permute-start(f32[48,48,1]{1,0,2:T(8,128)S(1)} %broadcast.1211), channel_id=1, source_target_pairs={{0,1},{2,3},{4,5},{6,7}} | collective-permute-start | bytes 27656 | tf_op jit(solution)/shard_map/ppermute | solution.py:41
  4.3 63.0 %collective-permute-start.149 = (f32[6,6,1]{2,1,0:T(8,128)S(1)}, f32[6,6,1]{2,1,0:T(8,128)S(1)}, u32[]{:S(2)}, u32[]{:S(2)}) collective-permute-start(f32[6,6,1]{2,1,0:T(8,128)S(1)} %broadcast.1247), channel_id=1, source_target_pairs={{1,0},{3,2},{5,4},{7,6}} | collective-permute-start | bytes 440 | tf_op jit(solution)/shard_map/ppermute | solution.py:42
  5.6 67.6 %collective-permute-start.148 = (f32[6,6,1]{2,1,0:T(8,128)S(1)}, f32[6,6,1]{2,1,0:T(8,128)S(1)}, u32[]{:S(2)}, u32[]{:S(2)}) collective-permute-start(f32[6,6,1]{2,1,0:T(8,128)S(1)} %broadcast.1247), channel_id=1, source_target_pairs={{0,1},{2,3},{4,5},{6,7}} | collective-permute-start | bytes 440 | tf_op jit(solution)/shard_map/ppermute | solution.py:41
  140.7 23.1 collective-permute-start.26
  142.6 21.1 collective-permute-start.27
  144.6 20.4 collective-permute-start.28
  216.6 26.9 collective-permute-start.34
  219.4 24.2 collective-permute-start.35
  220.7 23.7 collective-permute-start.32
  296.1 26.1 collective-permute-start.40
  298.6 23.7 collective-permute-start.41
  299.9 23.2 collective-permute-start.38
  374.8 26.3 collective-permute-start.46
  377.3 23.9 collective-permute-start.47
  378.6 23.4 collective-permute-start.44
  454.1 25.9 collective-permute-start.52
  456.5 23.4 collective-permute-start.53
  457.8 22.9 collective-permute-start.50
  726.6 19.1 collective-permute-start.62
  843.5 19.2 collective-permute-start.80
  2435.9 20.0 collective-permute-start.297
  2514.2 23.1 collective-permute-start.304
  2516.1 21.1 collective-permute-start.305
  2517.4 20.6 collective-permute-start.302
  2590.0 26.1 collective-permute-start.310
  2592.6 23.5 collective-permute-start.311
  2593.9 23.0 collective-permute-start.308
  2669.1 25.9 collective-permute-start.316
  2671.6 23.5 collective-permute-start.317
  2672.9 23.0 collective-permute-start.314
  2747.9 25.9 collective-permute-start.322
  2750.3 23.5 collective-permute-start.323
  2751.6 23.0 collective-permute-start.320
  2826.8 25.9 collective-permute-start.328
  2829.3 23.5 collective-permute-start.329
  2830.6 23.0 collective-permute-start.326
  2905.5 25.9 collective-permute-start.334
  2908.0 23.5 collective-permute-start.335
  2909.3 23.0 collective-permute-start.332
  2984.5 25.9 collective-permute-start.340
  2986.9 23.5 collective-permute-start.341
  2988.2 23.0 collective-permute-start.338
  3063.2 25.9 collective-permute-start.346
  3065.7 23.5 collective-permute-start.347
  3067.0 23.0 collective-permute-start.344
  3142.3 25.9 collective-permute-start.352
  3144.7 23.4 collective-permute-start.353
  3146.0 22.9 collective-permute-start.350
  3414.8 19.1 collective-permute-start.356
  5048.8 19.2 collective-permute-start.560
  5123.7 20.0 collective-permute-start.573
  5202.0 22.8 collective-permute-start.580
  5203.9 20.8 collective-permute-start.581
  5205.2 20.4 collective-permute-start.578
  5277.8 26.1 collective-permute-start.586
  5280.4 23.5 collective-permute-start.587
  5281.7 23.0 collective-permute-start.584
  5356.7 25.9 collective-permute-start.592
  5359.1 23.5 collective-permute-start.593
  5360.4 23.0 collective-permute-start.590
  5435.4 25.9 collective-permute-start.598
  5437.9 23.5 collective-permute-start.599
  5439.2 23.0 collective-permute-start.596
  (1301 other events, 13223.8 us)
where the time goes:
time: 5530 us; the launch traced here: 5490 us
  starting transfers between devices  2810 us (51%)
  local copies, waits for them, and re-layouts  1350 us (24%)
  other arithmetic  920 us (17%)
  waiting for transfers between devices  379 us (7%)
    ppermute x576, starting transfers between devices, halo_planes(): from_below = lax.ppermute(last, axis_name, upward)  2070 us
    ppermute x576, starting transfers between devices, halo_planes(): from_above = lax.ppermute(first, axis_name, downward)  747 us
    slice x534, local copies, waits for them, and re-layouts, shifted(): lax.slice_in_dim(grid, 1, extent, axis=axis)  362 us
    select_n x556, other arithmetic, halo_planes(): upper = jnp.where(position == count - 1, -last, from_above)  318 us
    reshape x10, local copies, waits for them, and re-layouts, restrict(): grid.reshape(grid_shape[0] // 2, 2, grid_shape[1] // 2, 2, grid_shape[2]...  299 us
    ppermute x576, waiting for transfers between devices, halo_planes(): from_above = lax.ppermute(first, axis_name, downward)  264 us
    slice x570, local copies, waits for them, and re-layouts, halo_planes(): first = lax.slice_in_dim(grid, 0, 1, axis=axis)  252 us
    select_n x88, other arithmetic, gs_sweep(): return jnp.where(red_cells, iterate, updated)  170 us

commit v1 on v0

v1 whole, which is shorter than its diff:
```python
import jax
import jax.numpy as jnp
from jax import lax
from jax.experimental import pallas as pl
from jax.experimental.pallas import tpu as pltpu
from jax.sharding import PartitionSpec as P

N = 192
CYCLES = 2
COARSE_SWEEPS = 24
F32 = jnp.float32
MESH = pl.DeviceIdType.MESH

PAIRS = (48, 24, 24, 12, 6, 3)
ROWS = (96, 48, 48, 24, 12, 6)
LANES = (96, 48, 48, 24, 12, 6)
ZO = (9, 7, 1, 1, 1, 1)
NZ = (66, 38, 26, 14, 8, 5)
YO = (24, 24, 8, 8, 8, 8)
NY = (144, 96, 64, 40, 32, 24)
ZHALO = (8, 6, 0, 0, 0, 0)
YHALO = (16, 16, 0, 0, 0, 0)
WINDOW = (112, 64, 48, 24, 16, 8)
UNROLL = (8, 10, 12, 12, 6, 3)
CHUNK = 16
SLOTS = 4
WIDTH = 128
TILE = 8
BRICK = 96
BOX = 24


def iotas(shape=(TILE, WIDTH)):
    return lax.broadcasted_iota(jnp.int32, shape, 0), lax.broadcasted_iota(jnp.int32, shape, 1)


class Level:
    def __init__(self, level, zi, yi, xi, m):
        self.level = level
        self.split = level < 2
        self.pairs, self.rows, self.lanes = PAIRS[level], ROWS[level], LANES[level]
        self.zo, self.yo = ZO[level], YO[level]
        self.planes = self.pairs + ZHALO[level]
        self.height = WINDOW[level]
        self.own_height = TILE * (-(-self.rows // TILE))
        if self.split:
            self.zs = self.zo - ZHALO[level] * zi
            self.ys = pl.multiple_of(self.yo - YHALO[level] * yi, TILE)
            self.own_at = pl.multiple_of(YHALO[level] * yi, TILE)
        else:
            self.zs, self.ys, self.own_at = self.zo, self.yo, 0
        self.zi = zi
        self.m = m
        self.row = pl.ds(self.ys, self.height)
        lane = lax.broadcasted_iota(jnp.int32, (TILE, WIDTH), 1)
        if self.split:
            self.valid = jnp.logical_or(lane < self.lanes + 16 * (1 - xi), lane >= WIDTH - 16 * xi)
            edges = (lane == (self.lanes - 1) * xi,)
        else:
            self.valid = lane < self.lanes
            edges = (lane == 0, lane == self.lanes - 1)
        self.outer = edges[0] if self.split else jnp.logical_or(*edges)
        self.w = jnp.where(self.valid, 1.0 / 6.0, 0.0).astype(F32)[None]
        sub, lane = iotas((self.height, WIDTH))
        if self.split:
            count = jnp.where(lane == (self.lanes - 1) * xi, 1.0, 0.0) + jnp.where(sub == (self.height - 1) * yi, 1.0, 0.0)
        else:
            count = (jnp.where(lane == 0, 1.0, 0.0) + jnp.where(lane == self.lanes - 1, 1.0, 0.0)
                     + jnp.where(sub == 0, 1.0, 0.0) + jnp.where(sub == self.rows - 1, 1.0, 0.0))
        m[...] = count.astype(F32)

    def odd(self, height, flip):
        sub, lane = iotas()
        return jnp.broadcast_to((lax.rem(sub + lane, 2) == (0 if flip else 1))[None], (height // TILE, TILE, WIDTH))

    def scaled(self, s):
        if self.rows % TILE and not self.split:
            sub, lane = iotas((self.height, WIDTH))
            inside = jnp.logical_and(sub < self.rows, lane < self.lanes)
            return s * jnp.where(inside, 1.0 / 6.0, 0.0).astype(F32)
        return flat(tiled(s) * self.w)


def tiled(v):
    return v.reshape(v.shape[0] // TILE, TILE, WIDTH)


def flat(v):
    return v.reshape(v.shape[0] * TILE, WIDTH)


def choose(mask, a, b):
    return flat(jnp.where(mask, tiled(a), tiled(b)))


def loop(count, body):
    def step(i, carry):
        body(i)
        return carry
    lax.fori_loop(0, count, step, 0)


def unrolled(count, body):
    def step(i, carry):
        body(i)
        return carry
    if count == 1:
        body(0)
    elif count > 1:
        lax.fori_loop(0, count, step, 0, unroll=True)


def grouped(count, group, body):
    if count == group:
        unrolled(group, body)
    else:
        loop(count // group, lambda i: unrolled(group, lambda k: body(i * group + k)))


def ghost_planes(dst, src, lv):
    pairs = [(lv.zo - 1, lv.zo), (lv.zo + lv.pairs, lv.zo + lv.pairs - 1)]
    if lv.split:
        pairs = [tuple(a + (b - a) * lv.zi for a, b in zip(*pairs))]
    for to, frm in pairs:
        dst[to, lv.row, :] = -src[frm, lv.row, :]


def gather_sum(a, b, hb, z, y, height, mask, m):
    row = pl.ds(y, height)
    bc = b[z, row, :]
    s = bc + choose(mask, b[z + 1, row, :], b[z - 1, row, :])
    s = s + (b[z, pl.ds(y - 1, height), :] + b[z, pl.ds(y + 1, height), :])
    s = s + (pltpu.roll(bc, 1, 1) + pltpu.roll(bc, 127, 1))
    av = a[z, row, :]
    return s + (hb[z, row, :] - m * av), av


def half_sweep(a, b, hb, lv, colour):
    ghost_planes(b, a, lv)
    mask = lv.odd(lv.height, colour)

    def plane(k):
        z = lv.zs + k
        s, _ = gather_sum(a, b, hb, z, lv.ys, lv.height, mask, lv.m[...])
        a[z, lv.row, :] = lv.scaled(s)
    grouped(lv.planes, UNROLL[lv.level], plane)


def sweep(u, hb, lv):
    half_sweep(u[0], u[1], hb[0], lv, 0)
    half_sweep(u[1], u[0], hb[1], lv, 1)


def zero_start(u, hb, lv):
    def clear(i):
        u[1][i] = jnp.zeros(u[1].shape[1:], F32)
    loop(u[1].shape[0], clear)

    def plane(k):
        u[0][lv.zs + k, lv.row, :] = lv.scaled(hb[0][lv.zs + k, lv.row, :])
    grouped(lv.planes, UNROLL[lv.level], plane)


def restrict(u, hb, lv, sums, coarse, coarse_at):
    height = lv.own_height
    group = TILE if lv.pairs % TILE == 0 else 6
    for c in range(2):
        ghost_planes(u[1 - c], u[c], lv)
        mask = lv.odd(height, c)

        def plane(k, c=c, mask=mask):
            s, v = gather_sum(u[c], u[1 - c], hb[c], lv.zo + k, lv.yo, height, mask, lv.m[pl.ds(lv.own_at, height), :])
            q = s - 6.0 * v
            sums[k, 0:height, :] = q if c == 0 else sums[k, 0:height, :] + q
        grouped(lv.pairs, group, plane)

    half = lv.lanes // 2
    rows = TILE * (-(-(lv.rows // 2) // TILE))
    sub, lane = iotas((rows, WIDTH))
    even_idx = jnp.minimum(2 * lane, 126)
    odd_idx = even_idx + 1
    scale = jnp.where(iotas()[1] < half, 0.5, 0.0).astype(F32)[None]
    mask = lv.odd(rows, 0)
    zc, yc = coarse_at

    def fold(pair):
        c = []
        for s in range(2):
            z = 2 * pair + s
            v = sums[z, pl.ds(0, rows, stride=2), :] + sums[z, pl.ds(1, rows, stride=2), :]
            v = jnp.take_along_axis(v, even_idx, axis=1) + jnp.take_along_axis(v, odd_idx, axis=1)
            c.append(flat(tiled(v) * scale))
        coarse[0][zc + pair, pl.ds(yc, rows), :] = choose(mask, c[1], c[0])
        coarse[1][zc + pair, pl.ds(yc, rows), :] = choose(mask, c[0], c[1])
    grouped(lv.pairs // 2, min(6, lv.pairs // 2), fold)


def prolong(u, e, lv, lc, yi, xi, cx, d):
    planes = lv.planes
    crows = (lv.rows + YHALO[lv.level]) // 2
    height = TILE * (-(-crows // TILE))
    if lv.level == 0:
        zc, yc, off = lc.zo - (ZHALO[0] // 2) * lv.zi, lc.yo - (YHALO[0] // 2) * yi, 0
    elif lv.level == 1:
        zc = lc.zo + (PAIRS[2] - planes // 2) * lv.zi
        yc = lc.yo + (ROWS[2] - crows) * yi
        off = (LANES[1] // 2) * xi
    else:
        zc, yc, off = lc.zo, lc.yo, 0
    if lv.split:
        yc = pl.multiple_of(yc, TILE)
    sub, lane = iotas((height, WIDTH))
    fine_lane = jnp.where(lane < 112, lane, lane - WIDTH) if lv.split else lane
    near = lax.div(fine_lane + WIDTH, 2) - 64
    far = near + jnp.where(lax.rem(lane, 2) == 1, 1, -1)
    if lv.split:
        far = jnp.where(lane == (lv.lanes - 1) * xi, near, far)
    else:
        far = jnp.where(jnp.logical_or(lane == 0, lane == lv.lanes - 1), near, far)
    idx_near = lax.rem(near + off + WIDTH, WIDTH)
    idx_far = lax.rem(far + off + WIDTH, WIDTH)
    w_near = jnp.where(lv.valid, 0.75, 0.0).astype(F32)[None]
    w_far = jnp.where(lv.valid, jnp.where(lv.outer, -0.25, 0.25), 0.0).astype(F32)[None]
    mask = lv.odd(height, 0)

    def along_x(pair):
        r, b = e[0][zc + pair, pl.ds(yc, height), :], e[1][zc + pair, pl.ds(yc, height), :]
        for s in range(2):
            c = choose(mask, b, r) if s == 0 else choose(mask, r, b)
            c = (tiled(jnp.take_along_axis(c, idx_near, axis=1)) * w_near
                 + tiled(jnp.take_along_axis(c, idx_far, axis=1)) * w_far)
            cx[2 * pair + s, TILE:TILE + height, :] = flat(c)
    pairs = planes // 2
    grouped(pairs, 7 if pairs % 7 == 0 else (5 if pairs % 5 == 0 else min(6, pairs)), along_x)

    if lv.split:
        sides = ((7 + (crows + 1) * yi, TILE + (crows - 1) * yi),)
    else:
        sides = ((7, TILE), (TILE + crows, 7 + crows))

    def edge_rows(z):
        for to, frm in sides:
            cx[z, pl.ds(to, 1), :] = -cx[z, pl.ds(frm, 1), :]
    grouped(planes, 2, edge_rows)

    def along_y(z):
        mid = 0.75 * cx[z, TILE:TILE + height, :]
        d[lv.zs + z, pl.ds(lv.ys, height, stride=2), :] = mid + 0.25 * cx[z, 7:7 + height, :]
        d[lv.zs + z, pl.ds(lv.ys + 1, height, stride=2), :] = mid + 0.25 * cx[z, 9:9 + height, :]
    grouped(planes, 2, along_y)
    ghost_planes(d, d, lv)
    mask = lv.odd(lv.height, 0)

    def along_z(k):
        z = lv.zs + k
        mid = 0.75 * d[z, lv.row, :]
        up, down = 0.25 * d[z + 1, lv.row, :], 0.25 * d[z - 1, lv.row, :]
        r = u[0][z, lv.row, :] + (mid + choose(mask, up, down))
        b = u[1][z, lv.row, :] + (mid + choose(mask, down, up))
        if not lv.split and lv.rows % TILE:
            keep = iotas((lv.height, WIDTH))[0] < lv.rows
            r, b = jnp.where(keep, r, 0.0), jnp.where(keep, b, 0.0)
        u[0][z, lv.row, :] = r
        u[1][z, lv.row, :] = b
    grouped(planes, 2, along_z)


def kernel(f_hbm, u_hbm, out_hbm, *scratch):
    (u0r, u0b, f0r, f0b, u1r, u1b, h1r, h1b, u2r, u2b, h2r, h2b, u3r, u3b, h3r, h3b, u4r, u4b, h4r, h4b,
     u5r, u5b, h5r, h5b, d0, d1, d2, d3, d4, cx0, cx1, cx2, cx3, cx4, t0, t1, t2, t3, t4,
     m0, m1, m2, m3, m4, m5, raw, xs, xr0, xr1, xs1, xr2, c2r, c2b, box, gbox,
     in_sem, out_sem, x_send, x_recv, send, recv, g_send, g_recv) = scratch
    zi, yi, xi = lax.axis_index('z'), lax.axis_index('y'), lax.axis_index('x')
    peers = ({'x': 1 - xi}, {'y': 1 - yi}, {'z': 1 - zi}, {'z': 1 - zi, 'y': 1 - yi})

    chunks = [(src, c) for src in (u_hbm, f_hbm) for c in range(BRICK // CHUNK)]

    def load(n):
        src, c = chunks[n]
        return pltpu.make_async_copy(src.at[pl.ds(c * CHUNK, CHUNK)], raw.at[n % SLOTS], in_sem.at[n % SLOTS])
    for n in range(SLOTS):
        load(n).start()

    for ref in (u0r, u0b, f0r, f0b, d0):
        def clear(i, ref=ref):
            ref[i] = jnp.zeros((NY[0], WIDTH), F32)
        loop(NZ[0], clear)
    for ref in (h1r.at[0], h1b.at[0], h1r.at[1], h1b.at[1], u1r, u1b, d1):
        def clear(i, ref=ref):
            ref[i] = jnp.zeros((NY[1], WIDTH), F32)
        loop(NZ[1], clear)
    for ref in (u2r, u2b, h2r, h2b, u3r, u3b, h3r, h3b, u4r, u4b, h4r, h4b, u5r, u5b, h5r, h5b, d2, d3, d4,
                cx0, cx1, cx2, cx3, cx4, t0, t1, t2, t3, t4, box):
        def clear(i, ref=ref):
            ref[i] = jnp.zeros(ref.shape[1:], F32)
        loop(ref.shape[0], clear)

    barrier = pltpu.get_barrier_semaphore()
    for peer in peers:
        pl.semaphore_signal(barrier, inc=1, device_id=peer, device_id_type=MESH)

    sub, lane = iotas((BRICK, BRICK))
    odd96 = lax.rem(sub + lane, 2) == 1
    h_sq = (1.0 / N) ** 2
    for n in range(len(chunks)):
        load(n).wait()
        slot = n % SLOTS
        first = n < len(chunks) // 2
        red, black = (u0r, u0b) if first else (f0r, f0b)
        start = ZO[0] + (n % (BRICK // CHUNK)) * (CHUNK // 2)

        def pack(i):
            p0, p1 = raw[slot, 2 * i], raw[slot, 2 * i + 1]
            r, b = jnp.where(odd96, p1, p0), jnp.where(odd96, p0, p1)
            if not first:
                r, b = r * h_sq, b * h_sq
            red[start + i, YO[0]:YO[0] + BRICK, 0:BRICK] = r
            black[start + i, YO[0]:YO[0] + BRICK, 0:BRICK] = b
        loop(CHUNK // 2, pack)
        if n + SLOTS < len(chunks):
            load(n + SLOTS).start()
    pl.semaphore_wait(barrier, len(peers))

    lvs = [Level(level, zi, yi, xi, m) for level, m in enumerate((m0, m1, m2, m3, m4, m5))]
    us = ((u0r, u0b), (u1r, u1b), (u2r, u2b), (u3r, u3b), (u4r, u4b), (u5r, u5b))
    ds_ = (d0, d1, d2, d3, d4)
    cxs = (cx0, cx1, cx2, cx3, cx4)
    ts = (t0, t1, t2, t3, t4)

    box_lane = lax.broadcasted_iota(jnp.int32, (BOX, WIDTH), 1)
    quarter = lax.div(box_lane, 32)

    def exchange_x(arrays, lv, s_buf, r_buf, sem_at):
        row = pl.ds(lv.yo, lv.rows)
        wide = lax.broadcasted_iota(jnp.int32, (lv.rows, WIDTH), 1)
        group = lax.div(wide, 16)
        from_lane = (lv.lanes - 16) * (1 - xi)
        to_lane = lv.lanes + (112 - lv.lanes) * xi
        copies = []
        for n, a in enumerate(arrays):
            def pack_x(i, a=a, n=n):
                acc = None
                for k in range(TILE):
                    v = pltpu.roll(a[lv.zo + TILE * i + k, row, :], lax.rem(16 * k + WIDTH - from_lane, WIDTH), 1)
                    acc = v if k == 0 else jnp.where(group == k, v, acc)
                s_buf[n, i] = acc
            loop(lv.pairs // TILE, pack_x)
            copy = pltpu.make_async_remote_copy(
                src_ref=s_buf.at[n], dst_ref=r_buf.at[n], send_sem=x_send.at[sem_at + n], recv_sem=x_recv.at[sem_at + n],
                device_id=peers[0], device_id_type=MESH)
            copy.start()
            copies.append(copy)
        inside = jnp.logical_and(wide >= to_lane, wide < to_lane + 16)
        for n, a in enumerate(arrays):
            copies[n].wait()

            def unpack_x(i, a=a, n=n):
                acc = r_buf[n, i]
                for k in range(TILE):
                    z = lv.zo + TILE * i + k
                    v = pltpu.roll(acc, lax.rem(to_lane + WIDTH - 16 * k, WIDTH), 1)
                    a[z, row, :] = jnp.where(inside, v, a[z, row, :])
            loop(lv.pairs // TILE, unpack_x)

    def send_faces(specs, lv, sem_at):
        copies = []
        for a, zn, yn in specs:
            z_own, y_own = pl.ds(lv.zo, lv.pairs), pl.ds(lv.yo, lv.rows)
            y_in = pl.multiple_of(lv.yo + (lv.rows - yn) * (1 - yi), TILE)
            y_to = pl.multiple_of(lv.yo - yn + (lv.rows + yn) * yi, TILE)
            z_in = lv.zo + (lv.pairs - zn) * (1 - zi)
            z_to = lv.zo - zn + (lv.pairs + zn) * zi
            parts = (
                ((z_own, pl.ds(y_in, yn)), (z_own, pl.ds(y_to, yn)), peers[1]),
                ((pl.ds(z_in, zn), y_own), (pl.ds(z_to, zn), y_own), peers[2]),
                ((pl.ds(z_in, zn), pl.ds(y_in, yn)), (pl.ds(z_to, zn), pl.ds(y_to, yn)), peers[3]),
            )
            for src, dst, peer in parts:
                at = sem_at + len(copies)
                copy = pltpu.make_async_remote_copy(
                    src_ref=a.at[src[0], src[1]], dst_ref=a.at[dst[0], dst[1]], send_sem=send.at[at], recv_sem=recv.at[at],
                    device_id=peer, device_id_type=MESH)
                copy.start()
                copies.append(copy)
        return copies

    def gather_level2(cycle):
        def pack_box(i):
            for c, a in enumerate((c2r, c2b)):
                acc = a[4 * i]
                for k in range(1, 4):
                    acc = jnp.where(quarter == k, pltpu.roll(a[4 * i + k], 32 * k, 1), acc)
                box[cycle, c, i] = acc
        loop(3, pack_box)
        me = 4 * xi + 2 * zi + yi
        copies = []
        for n, peer in enumerate(peers):
            copy = pltpu.make_async_remote_copy(
                src_ref=box.at[cycle], dst_ref=gbox.at[cycle, me], send_sem=g_send.at[cycle, n], recv_sem=g_recv.at[cycle, n],
                device_id=peer, device_id_type=MESH)
            copy.start()
            copies.append(copy)
        for n, (dz, dy) in ((1, (0, 1)), (2, (1, 0)), (3, (1, 1))):
            copies[n].wait_recv()
            sz, sy = zi + dz - 2 * dz * zi, yi + dy - 2 * dy * yi
            at = 4 * xi + 2 * sz + sy
            copy = pltpu.make_async_remote_copy(
                src_ref=gbox.at[cycle, at], dst_ref=gbox.at[cycle, at], send_sem=g_send.at[cycle, 3 + n],
                recv_sem=g_recv.at[cycle, 3 + n], device_id=peers[0], device_id_type=MESH)
            copy.start()
            copies.append(copy)
        copies[0].wait_recv()
        for copy in copies[:4]:
            copy.wait_send()
        for copy in copies[4:]:
            copy.wait()
        for c, a in enumerate((c2r, c2b)):
            gbox[cycle, me, c] = box[cycle, c]

        def unpack_box(i):
            for c, a in enumerate((h2r, h2b)):
                for q in range(4):
                    sz, sy = divmod(q, 2)
                    lo, hi = gbox[cycle, q, c, i], gbox[cycle, 4 + q, c, i]
                    for k in range(4):
                        lower = pltpu.roll(lo, WIDTH - 32 * k, 1) if k else lo
                        upper = pltpu.roll(hi, (152 - 32 * k) % WIDTH, 1)
                        v = jnp.where(box_lane < BOX, lower, jnp.where(box_lane < 48, upper, 0.0))
                        a[ZO[2] + 12 * sz + 4 * i + k, YO[2] + BOX * sy:YO[2] + BOX * sy + BOX, :] = v
        loop(3, unpack_box)

    l0 = lvs[0]
    exchange_x((u0r, u0b, f0r, f0b), l0, xs, xr0, 0)
    for copy in send_faces(((u0r, 2, TILE), (u0b, 3, TILE), (f0r, 4, TILE), (f0b, 4, TILE)), l0, 0):
        copy.wait()

    def v_cycle(cycle):
        h1 = (h1r.at[cycle], h1b.at[cycle])
        hs = ((f0r, f0b), h1, (h2r, h2b), (h3r, h3b), (h4r, h4b), (h5r, h5b))
        l1 = lvs[1]
        loop(2, lambda i: sweep(us[0], hs[0], l0))
        restrict(us[0], hs[0], l0, ts[0], h1, (ZO[1], YO[1]))
        exchange_x(h1, l1, xs1, xr2.at[cycle], TILE)
        for copy in send_faces(((h1[0], 6, 16), (h1[1], 6, 16)), l1, 12):
            copy.wait()
        for level in range(1, 5):
            lv = lvs[level]
            zero_start(us[level], hs[level], lv)
            half_sweep(us[level][1], us[level][0], hs[level][1], lv, 1)
            sweep(us[level], hs[level], lv)
            if level == 1:
                restrict(us[1], h1, l1, ts[1], (c2r, c2b), (0, 0))
                gather_level2(cycle)
                exchange_x(us[0], l0, xs, xr1.at[cycle], 4)
                pending = send_faces(((u0r, 4, TILE), (u0b, 5, 16)), l0, 18)
            else:
                restrict(us[level], hs[level], lv, ts[level], hs[level + 1], (ZO[level + 1], YO[level + 1]))
        lv = lvs[5]
        zero_start(us[5], hs[5], lv)
        half_sweep(us[5][1], us[5][0], hs[5][1], lv, 1)
        loop(COARSE_SWEEPS - 1, lambda i: sweep(us[5], hs[5], lvs[5]))
        for level in range(4, -1, -1):
            lv = lvs[level]
            if level == 0:
                for copy in pending:
                    copy.wait()
            prolong(us[level], us[level + 1], lv, lvs[level + 1], yi, xi, cxs[level], ds_[level])
            loop(2, lambda i, lv=lv, level=level: sweep(us[level], hs[level], lv))
    loop(CYCLES, v_cycle)

    stores = []
    for n in range(BRICK // CHUNK):
        slot = n % SLOTS
        if n >= SLOTS:
            stores[n - SLOTS].wait()

        def unpack(i):
            z = ZO[0] + n * (CHUNK // 2) + i
            r, b = u0r[z, YO[0]:YO[0] + BRICK, 0:BRICK], u0b[z, YO[0]:YO[0] + BRICK, 0:BRICK]
            raw[slot, 2 * i] = jnp.where(odd96, b, r)
            raw[slot, 2 * i + 1] = jnp.where(odd96, r, b)
        loop(CHUNK // 2, unpack)
        copy = pltpu.make_async_copy(raw.at[slot], out_hbm.at[pl.ds(n * CHUNK, CHUNK)], out_sem.at[slot])
        copy.start()
        stores.append(copy)
    for copy in stores[-SLOTS:]:
        copy.wait()


def vmem(*shape):
    return pltpu.VMEM(shape, F32)


def scratch_shapes():
    arr = [vmem(NZ[level], NY[level], WIDTH) for level in range(6)]
    shapes = [arr[0]] * 4 + [arr[1]] * 2 + [vmem(2, NZ[1], NY[1], WIDTH)] * 2
    for level in range(2, 6):
        shapes += [arr[level]] * 4
    shapes += arr[:5]
    shapes += [vmem(56, 80, WIDTH), vmem(30, 48, WIDTH), vmem(BOX, 40, WIDTH), vmem(12, 32, WIDTH), vmem(6, BOX, WIDTH)]
    shapes += [vmem(48, BRICK, WIDTH), vmem(BOX, 48, WIDTH), vmem(BOX, 48, WIDTH), vmem(12, 32, WIDTH), vmem(6, 16, WIDTH)]
    shapes += [vmem(height, WIDTH) for height in WINDOW]
    shapes += [vmem(SLOTS, CHUNK, BRICK, BRICK)]
    shapes += [vmem(4, 6, BRICK, WIDTH), vmem(4, 6, BRICK, WIDTH), vmem(2, 2, 6, BRICK, WIDTH)]
    shapes += [vmem(2, 3, 48, WIDTH), vmem(2, 2, 3, 48, WIDTH)]
    shapes += [vmem(12, BOX, WIDTH), vmem(12, BOX, WIDTH), vmem(2, 2, 3, BOX, WIDTH), vmem(2, TILE, 2, 3, BOX, WIDTH)]
    dma = pltpu.SemaphoreType.DMA
    shapes += [dma((SLOTS,)), dma((SLOTS,)), dma((10,)), dma((10,)), dma((BOX,)), dma((BOX,)), dma((2, 7)), dma((2, 7))]
    return shapes


def solution(mesh):
    spec = P(('batch', 'z'), 'y', 'x')

    def local_solve(source, initial_guess):
        return pl.pallas_call(
            kernel,
            out_shape=jax.ShapeDtypeStruct(source.shape, F32),
            in_specs=[pl.BlockSpec(memory_space=pl.ANY)] * 2,
            out_specs=pl.BlockSpec(memory_space=pl.ANY),
            scratch_shapes=scratch_shapes(),
            compiler_params=pltpu.CompilerParams(collective_id=0, has_side_effects=True, vmem_limit_bytes=67043328),
            name='multigrid',
        )(source, initial_guess)

    return jax.shard_map(local_solve, mesh=mesh, in_specs=(spec, spec), out_specs=spec, check_vma=False)
```

time: 5530 us -> 203 us (0.04)
  starting transfers between devices: 2810 us -> 0 us
  local copies, waits for them, and re-layouts: 1350 us -> 4.84 us
  other arithmetic: 920 us -> 0 us
  waiting for transfers between devices: 379 us -> 0 us
  Pallas kernels: 0 us -> 198 us
    ppermute x1152 -> x0, starting transfers between devices: 2810 us -> none  [the longest x576 2070 us: halo_planes(): from_below = lax.ppermute(last, axis_name, upward)]
    slice x1186 -> x0, local copies, waits for them, and re-layouts: 729 us -> none  [the longest x534 362 us: shifted(): lax.slice_in_dim(grid, 1, extent, axis=axis)]
    select_n x764 -> x0, other arithmetic: 664 us -> none  [the longest x556 318 us: halo_planes(): upper = jnp.where(position == count - 1, -last, from_above)]
    ppermute x1152 -> x0, waiting for transfers between devices: 379 us -> none  [the longest x576 264 us: halo_planes(): from_above = lax.ppermute(first, axis_name, downward)]
    reshape x32 -> x0, local copies, waits for them, and re-layouts: 320 us -> none  [the longest x10 299 us: restrict(): grid.reshape(grid_shape[0] // 2, 2, grid_shape[1] // 2, 2, grid_shape[2]...]
    pallas_call x0 -> x1, Pallas kernels: none -> 198 us  [local_solve(): pl.pallas_call(kernel, out_shape=jax.ShapeDtypeStruct(source.shape, F32),...]
    ppermute x74 -> x0, local copies, waits for them, and re-layouts: 181 us -> none  [the longest x37 97.6 us: halo_planes(): from_above = lax.ppermute(first, axis_name, downward)]
    reduce_sum x10 -> x0, other arithmetic: 165 us -> none  [restrict(): return folded.mean(axis=(1, 3, 5))]
where the time goes in v1:
time: 203 us
  Pallas kernels  198 us (98%)
  local copies, waits for them, and re-layouts  4.84 us (2%)
    pallas_call x1, Pallas kernels, local_solve(): pl.pallas_call(kernel, out_shape=jax.ShapeDtypeStruct(source.shape, F32),...  198 us
    unnamed x1, local copies, waits for them, and re-layouts  4.84 us

profile of v1, /device:TPU:0, one launch (start us, length us, event | category | flops | bytes accessed | tf_op | source)
XLA Modules:
  0.0 203.1 jit_solution(16865308709519149158)
XLA Ops:
  0.0 198.3 %multigrid.1 = f32[96,96,96]{2,1,0:T(8,128)} custom-call(f32[96,96,96]{2,1,0:T(8,128)} %f_hbm.1, f32[96,96,96]{2,1,0:T(8,128)} %u_hbm.1), custom_call_target="tpu_custom_call" | custom-call | tf_op jit(solution)/shard_map/multigrid/pallas_call | solution.py:516
  198.3 4.8 %copy.4 = f32[96,96,96]{2,1,0:T(8,128)} copy(f32[96,96,96]{2,1,0:T(8,128)} %multigrid.1) | data formatting | bytes 7077888

commit v2 on v1

--- a/solution.py
+++ b/solution.py
@@ -28,6 +28,7 @@
 TILE = 8
 BRICK = 96
 BOX = 24
+XHALO = 16
 
 
 def iotas(shape=(TILE, WIDTH)):
@@ -54,7 +55,7 @@
         self.row = pl.ds(self.ys, self.height)
         lane = lax.broadcasted_iota(jnp.int32, (TILE, WIDTH), 1)
         if self.split:
-            self.valid = jnp.logical_or(lane < self.lanes + 16 * (1 - xi), lane >= WIDTH - 16 * xi)
+            self.valid = jnp.logical_or(lane < self.lanes + XHALO * (1 - xi), lane >= WIDTH - XHALO * xi)
             edges = (lane == (self.lanes - 1) * xi,)
         else:
             self.valid = lane < self.lanes
@@ -63,10 +64,10 @@
         self.w = jnp.where(self.valid, 1.0 / 6.0, 0.0).astype(F32)[None]
         sub, lane = iotas((self.height, WIDTH))
         if self.split:
-            count = jnp.where(lane == (self.lanes - 1) * xi, 1.0, 0.0) + jnp.where(sub == (self.height - 1) * yi, 1.0, 0.0)
+            count = ones(lane == (self.lanes - 1) * xi) + ones(sub == (self.height - 1) * yi)
         else:
-            count = (jnp.where(lane == 0, 1.0, 0.0) + jnp.where(lane == self.lanes - 1, 1.0, 0.0)
-                     + jnp.where(sub == 0, 1.0, 0.0) + jnp.where(sub == self.rows - 1, 1.0, 0.0))
+            count = (ones(lane == 0) + ones(lane == self.lanes - 1)
+                     + ones(sub == 0) + ones(sub == self.rows - 1))
         m[...] = count.astype(F32)
 
     def odd(self, height, flip):
@@ -79,6 +80,18 @@
             inside = jnp.logical_and(sub < self.rows, lane < self.lanes)
             return s * jnp.where(inside, 1.0 / 6.0, 0.0).astype(F32)
         return flat(tiled(s) * self.w)
+
+
+def turn(v, by):
+    return pltpu.roll(v, by, 1)
+
+
+def pick(v, idx):
+    return jnp.take_along_axis(v, idx, axis=1)
+
+
+def ones(where):
+    return jnp.where(where, 1.0, 0.0)
 
 
 def tiled(v):
@@ -130,7 +143,7 @@
     bc = b[z, row, :]
     s = bc + choose(mask, b[z + 1, row, :], b[z - 1, row, :])
     s = s + (b[z, pl.ds(y - 1, height), :] + b[z, pl.ds(y + 1, height), :])
-    s = s + (pltpu.roll(bc, 1, 1) + pltpu.roll(bc, 127, 1))
+    s = s + (turn(bc, 1) + turn(bc, WIDTH - 1))
     av = a[z, row, :]
     return s + (hb[z, row, :] - m * av), av
 
@@ -188,7 +201,7 @@
         for s in range(2):
             z = 2 * pair + s
             v = sums[z, pl.ds(0, rows, stride=2), :] + sums[z, pl.ds(1, rows, stride=2), :]
-            v = jnp.take_along_axis(v, even_idx, axis=1) + jnp.take_along_axis(v, odd_idx, axis=1)
+            v = pick(v, even_idx) + pick(v, odd_idx)
             c.append(flat(tiled(v) * scale))
         coarse[0][zc + pair, pl.ds(yc, rows), :] = choose(mask, c[1], c[0])
         coarse[1][zc + pair, pl.ds(yc, rows), :] = choose(mask, c[0], c[1])
@@ -227,8 +240,8 @@
         r, b = e[0][zc + pair, pl.ds(yc, height), :], e[1][zc + pair, pl.ds(yc, height), :]
         for s in range(2):
             c = choose(mask, b, r) if s == 0 else choose(mask, r, b)
-            c = (tiled(jnp.take_along_axis(c, idx_near, axis=1)) * w_near
-                 + tiled(jnp.take_along_axis(c, idx_far, axis=1)) * w_far)
+            c = (tiled(pick(c, idx_near)) * w_near
+                 + tiled(pick(c, idx_far)) * w_far)
             cx[2 * pair + s, TILE:TILE + height, :] = flat(c)
     pairs = planes // 2
     grouped(pairs, 7 if pairs % 7 == 0 else (5 if pairs % 5 == 0 else min(6, pairs)), along_x)
@@ -330,44 +343,50 @@
     box_lane = lax.broadcasted_iota(jnp.int32, (BOX, WIDTH), 1)
     quarter = lax.div(box_lane, 32)
 
-    def exchange_x(arrays, lv, s_buf, r_buf, sem_at):
-        row = pl.ds(lv.yo, lv.rows)
-        wide = lax.broadcasted_iota(jnp.int32, (lv.rows, WIDTH), 1)
-        group = lax.div(wide, 16)
-        from_lane = (lv.lanes - 16) * (1 - xi)
-        to_lane = lv.lanes + (112 - lv.lanes) * xi
-        copies = []
-        for n, a in enumerate(arrays):
-            def pack_x(i, a=a, n=n):
-                acc = None
-                for k in range(TILE):
-                    v = pltpu.roll(a[lv.zo + TILE * i + k, row, :], lax.rem(16 * k + WIDTH - from_lane, WIDTH), 1)
-                    acc = v if k == 0 else jnp.where(group == k, v, acc)
-                s_buf[n, i] = acc
-            loop(lv.pairs // TILE, pack_x)
-            copy = pltpu.make_async_remote_copy(
-                src_ref=s_buf.at[n], dst_ref=r_buf.at[n], send_sem=x_send.at[sem_at + n], recv_sem=x_recv.at[sem_at + n],
-                device_id=peers[0], device_id_type=MESH)
-            copy.start()
-            copies.append(copy)
-        inside = jnp.logical_and(wide >= to_lane, wide < to_lane + 16)
-        for n, a in enumerate(arrays):
-            copies[n].wait()
-
-            def unpack_x(i, a=a, n=n):
-                acc = r_buf[n, i]
-                for k in range(TILE):
-                    z = lv.zo + TILE * i + k
-                    v = pltpu.roll(acc, lax.rem(to_lane + WIDTH - 16 * k, WIDTH), 1)
-                    a[z, row, :] = jnp.where(inside, v, a[z, row, :])
-            loop(lv.pairs // TILE, unpack_x)
-
-    def send_faces(specs, lv, sem_at):
+    class Columns:
+        def __init__(self, arrays, lv, s_buf, r_buf, sem_at):
+            self.arrays, self.lv, self.r_buf = arrays, lv, r_buf
+            self.wide = lax.broadcasted_iota(jnp.int32, (lv.rows, WIDTH), 1)
+            self.row = pl.ds(lv.yo, lv.rows)
+            group = lax.div(self.wide, XHALO)
+            from_lane = (lv.lanes - XHALO) * (1 - xi)
+            self.copies = []
+            for n, a in enumerate(arrays):
+                def pack_x(i, a=a, n=n):
+                    acc = None
+                    for k in range(TILE):
+                        v = turn(a[lv.zo + TILE * i + k, self.row, :], lax.rem(XHALO * k + WIDTH - from_lane, WIDTH))
+                        acc = v if k == 0 else jnp.where(group == k, v, acc)
+                    s_buf[n, i] = acc
+                loop(lv.pairs // TILE, pack_x)
+                at = sem_at + n
+                copy = pltpu.make_async_remote_copy(
+                    src_ref=s_buf.at[n], dst_ref=r_buf.at[n], send_sem=x_send.at[at], recv_sem=x_recv.at[at],
+                    device_id=peers[0], device_id_type=MESH)
+                copy.start()
+                self.copies.append(copy)
+
+        def finish(self):
+            lv, row = self.lv, self.row
+            to_lane = lv.lanes + (112 - lv.lanes) * xi
+            inside = jnp.logical_and(self.wide >= to_lane, self.wide < to_lane + XHALO)
+            for n, a in enumerate(self.arrays):
+                self.copies[n].wait()
+
+                def unpack_x(i, a=a, n=n):
+                    acc = self.r_buf[n, i]
+                    for k in range(TILE):
+                        z = lv.zo + TILE * i + k
+                        v = turn(acc, lax.rem(to_lane + WIDTH - XHALO * k, WIDTH))
+                        a[z, row, :] = jnp.where(inside, v, a[z, row, :])
+                loop(lv.pairs // TILE, unpack_x)
+
+    def send_faces(specs, lv, sem_at, start=True):
         copies = []
         for a, zn, yn in specs:
             z_own, y_own = pl.ds(lv.zo, lv.pairs), pl.ds(lv.yo, lv.rows)
-            y_in = pl.multiple_of(lv.yo + (lv.rows - yn) * (1 - yi), TILE)
-            y_to = pl.multiple_of(lv.yo - yn + (lv.rows + yn) * yi, TILE)
+            y_in = lv.yo + (lv.rows - yn) * (1 - yi)
+            y_to = lv.yo - yn + (lv.rows + yn) * yi
             z_in = lv.zo + (lv.pairs - zn) * (1 - zi)
             z_to = lv.zo - zn + (lv.pairs + zn) * zi
             parts = (
@@ -380,7 +399,8 @@
                 copy = pltpu.make_async_remote_copy(
                     src_ref=a.at[src[0], src[1]], dst_ref=a.at[dst[0], dst[1]], send_sem=send.at[at], recv_sem=recv.at[at],
                     device_id=peer, device_id_type=MESH)
-                copy.start()
+                if start:
+                    copy.start()
                 copies.append(copy)
         return copies
 
@@ -389,7 +409,7 @@
             for c, a in enumerate((c2r, c2b)):
                 acc = a[4 * i]
                 for k in range(1, 4):
-                    acc = jnp.where(quarter == k, pltpu.roll(a[4 * i + k], 32 * k, 1), acc)
+                    acc = jnp.where(quarter == k, turn(a[4 * i + k], 32 * k), acc)
                 box[cycle, c, i] = acc
         loop(3, pack_box)
         me = 4 * xi + 2 * zi + yi
@@ -423,15 +443,20 @@
                     sz, sy = divmod(q, 2)
                     lo, hi = gbox[cycle, q, c, i], gbox[cycle, 4 + q, c, i]
                     for k in range(4):
-                        lower = pltpu.roll(lo, WIDTH - 32 * k, 1) if k else lo
-                        upper = pltpu.roll(hi, (152 - 32 * k) % WIDTH, 1)
+                        lower = turn(lo, WIDTH - 32 * k) if k else lo
+                        upper = turn(hi, (152 - 32 * k) % WIDTH)
                         v = jnp.where(box_lane < BOX, lower, jnp.where(box_lane < 48, upper, 0.0))
                         a[ZO[2] + 12 * sz + 4 * i + k, YO[2] + BOX * sy:YO[2] + BOX * sy + BOX, :] = v
         loop(3, unpack_box)
 
     l0 = lvs[0]
-    exchange_x((u0r, u0b, f0r, f0b), l0, xs, xr0, 0)
-    for copy in send_faces(((u0r, 2, TILE), (u0b, 3, TILE), (f0r, 4, TILE), (f0b, 4, TILE)), l0, 0):
+    x_u = Columns((u0r, u0b), l0, xs, xr0, 0)
+    x_f = Columns((f0r, f0b), l0, xs.at[2:4], xr0.at[2:4], 2)
+    x_u.finish()
+    faces = send_faces(((u0r, 2, 4), (u0b, 3, 5)), l0, 0)
+    x_f.finish()
+    faces += send_faces(((f0r, 2, 4), (f0b, 2, 4)), l0, 6)
+    for copy in faces:
         copy.wait()
 
     def v_cycle(cycle):
@@ -440,8 +465,10 @@
         l1 = lvs[1]
         loop(2, lambda i: sweep(us[0], hs[0], l0))
         restrict(us[0], hs[0], l0, ts[0], h1, (ZO[1], YO[1]))
-        exchange_x(h1, l1, xs1, xr2.at[cycle], TILE)
-        for copy in send_faces(((h1[0], 6, 16), (h1[1], 6, 16)), l1, 12):
+        Columns(h1, l1, xs1, xr2.at[cycle], TILE).finish()
+        faces = send_faces(((h1[0], 6, 12), (h1[1], 6, 12)), l1, 12)
+        Columns(us[0], l0, xs, xr1.at[cycle], 4).finish()
+        for copy in faces:
             copy.wait()
         for level in range(1, 5):
             lv = lvs[level]
@@ -451,8 +478,11 @@
             if level == 1:
                 restrict(us[1], h1, l1, ts[1], (c2r, c2b), (0, 0))
                 gather_level2(cycle)
-                exchange_x(us[0], l0, xs, xr1.at[cycle], 4)
-                pending = send_faces(((u0r, 4, TILE), (u0b, 5, 16)), l0, 18)
+                pending = send_faces(((u0r, 4, TILE), (u0b, 5, 9)), l0, 18)
+
+                @pl.when(cycle == 0)
+                def deeper_source():
+                    send_faces(((f0r, 4, TILE), (f0b, 4, TILE)), l0, 0)
             else:
                 restrict(us[level], hs[level], lv, ts[level], hs[level + 1], (ZO[level + 1], YO[level + 1]))
         lv = lvs[5]
@@ -464,6 +494,11 @@
             if level == 0:
                 for copy in pending:
                     copy.wait()
+
+                @pl.when(cycle == 0)
+                def deeper_source_arrived():
+                    for copy in send_faces(((f0r, 4, TILE), (f0b, 4, TILE)), l0, 0, False):
+                        copy.wait()
             prolong(us[level], us[level + 1], lv, lvs[level + 1], yi, xi, cxs[level], ds_[level])
             loop(2, lambda i, lv=lv, level=level: sweep(us[level], hs[level], lv))
     loop(CYCLES, v_cycle)
@@ -498,7 +533,7 @@
         shapes += [arr[level]] * 4
     shapes += arr[:5]
     shapes += [vmem(56, 80, WIDTH), vmem(30, 48, WIDTH), vmem(BOX, 40, WIDTH), vmem(12, 32, WIDTH), vmem(6, BOX, WIDTH)]
-    shapes += [vmem(48, BRICK, WIDTH), vmem(BOX, 48, WIDTH), vmem(BOX, 48, WIDTH), vmem(12, 32, WIDTH), vmem(6, 16, WIDTH)]
+    shapes += [vmem(48, BRICK, WIDTH), vmem(BOX, 48, WIDTH), vmem(BOX, 48, WIDTH), vmem(12, 32, WIDTH), vmem(6, XHALO, WIDTH)]
     shapes += [vmem(height, WIDTH) for height in WINDOW]
     shapes += [vmem(SLOTS, CHUNK, BRICK, BRICK)]
     shapes += [vmem(4, 6, BRICK, WIDTH), vmem(4, 6, BRICK, WIDTH), vmem(2, 2, 6, BRICK, WIDTH)]

time: 203 us -> 184 us (0.906)
  Pallas kernels: 198 us -> 179 us
    pallas_call x1, Pallas kernels: 198 us -> 179 us  [local_solve(): pl.pallas_call(kernel, out_shape=jax.ShapeDtypeStruct(source.shape, F32),...]
where the time goes in v2:
time: 184 us; the launch traced here: 183 us
  Pallas kernels  179 us (97%)
  local copies, waits for them, and re-layouts  4.84 us (3%)
    pallas_call x1, Pallas kernels, local_solve(): pl.pallas_call(kernel, out_shape=jax.ShapeDtypeStruct(source.shape, F32),...  179 us
    unnamed x1, local copies, waits for them, and re-layouts  4.84 us

profile of v2, /device:TPU:0, one launch (start us, length us, event | category | flops | bytes accessed | tf_op | source)
XLA Modules:
  0.0 183.5 jit_solution(13545489756078758032)
XLA Ops:
  0.0 178.6 %multigrid.1 = f32[96,96,96]{2,1,0:T(8,128)} custom-call(f32[96,96,96]{2,1,0:T(8,128)} %f_hbm.1, f32[96,96,96]{2,1,0:T(8,128)} %u_hbm.1), custom_call_target="tpu_custom_call" | custom-call | tf_op jit(solution)/shard_map/multigrid/pallas_call | solution.py:551
  178.6 4.8 %copy.4 = f32[96,96,96]{2,1,0:T(8,128)} copy(f32[96,96,96]{2,1,0:T(8,128)} %multigrid.1) | data formatting | bytes 7077888

commit v3 on v2

--- a/solution.py
+++ b/solution.py
@@ -29,6 +29,7 @@
 BRICK = 96
 BOX = 24
 XHALO = 16
+DEEP = 12
 
 
 def iotas(shape=(TILE, WIDTH)):
@@ -51,6 +52,8 @@
         else:
             self.zs, self.ys, self.own_at = self.zo, self.yo, 0
         self.zi = zi
+        self.side = zi.astype(F32)
+        self.z_at = self.zo - self.zs
         self.m = m
         self.row = pl.ds(self.ys, self.height)
         lane = lax.broadcasted_iota(jnp.int32, (TILE, WIDTH), 1)
@@ -70,6 +73,12 @@
                      + ones(sub == 0) + ones(sub == self.rows - 1))
         m[...] = count.astype(F32)
 
+    def ghosts(self):
+        low, high = (self.zo - 1, self.zo), (self.zo + self.pairs, self.zo + self.pairs - 1)
+        if self.split:
+            return [tuple(a + (b - a) * self.zi for a, b in zip(low, high))]
+        return [low, high]
+
     def odd(self, height, flip):
         sub, lane = iotas()
         return jnp.broadcast_to((lax.rem(sub + lane, 2) == (0 if flip else 1))[None], (height // TILE, TILE, WIDTH))
@@ -131,10 +140,7 @@
 
 
 def ghost_planes(dst, src, lv):
-    pairs = [(lv.zo - 1, lv.zo), (lv.zo + lv.pairs, lv.zo + lv.pairs - 1)]
-    if lv.split:
-        pairs = [tuple(a + (b - a) * lv.zi for a, b in zip(*pairs))]
-    for to, frm in pairs:
+    for to, frm in lv.ghosts():
         dst[to, lv.row, :] = -src[frm, lv.row, :]
 
 
@@ -148,20 +154,34 @@
     return s + (hb[z, row, :] - m * av), av
 
 
-def half_sweep(a, b, hb, lv, colour):
+def half_sweep(a, b, hb, lv, colour, sums=None):
     ghost_planes(b, a, lv)
     mask = lv.odd(lv.height, colour)
 
     def plane(k):
         z = lv.zs + k
-        s, _ = gather_sum(a, b, hb, z, lv.ys, lv.height, mask, lv.m[...])
-        a[z, lv.row, :] = lv.scaled(s)
+        m = lv.m[...]
+        s, old = gather_sum(a, b, hb, z, lv.ys, lv.height, mask, m)
+        new = lv.scaled(s)
+        a[z, lv.row, :] = new
+        if sums is not None:
+            sums[k, 0:lv.height, :] = m * (old - new)
     grouped(lv.planes, UNROLL[lv.level], plane)
+    if sums is not None:
+        for n, (to, frm) in enumerate(lv.ghosts()):
+            delta = -(a[frm, lv.row, :] + b[to, lv.row, :])
+            up = lv.side if lv.split else float(n)
+            k = frm - lv.zs
+            sums[k, 0:lv.height, :] = sums[k, 0:lv.height, :] + choose(mask, delta * up, delta * (1.0 - up))
+
+
+def relax(u, hb, lv, colour, sums=None):
+    half_sweep(u[colour], u[1 - colour], hb[colour], lv, colour, sums)
 
 
 def sweep(u, hb, lv):
-    half_sweep(u[0], u[1], hb[0], lv, 0)
-    half_sweep(u[1], u[0], hb[1], lv, 1)
+    relax(u, hb, lv, 0)
+    relax(u, hb, lv, 1)
 
 
 def zero_start(u, hb, lv):
@@ -176,16 +196,14 @@
 
 def restrict(u, hb, lv, sums, coarse, coarse_at):
     height = lv.own_height
-    group = TILE if lv.pairs % TILE == 0 else 6
-    for c in range(2):
-        ghost_planes(u[1 - c], u[c], lv)
-        mask = lv.odd(height, c)
-
-        def plane(k, c=c, mask=mask):
-            s, v = gather_sum(u[c], u[1 - c], hb[c], lv.zo + k, lv.yo, height, mask, lv.m[pl.ds(lv.own_at, height), :])
-            q = s - 6.0 * v
-            sums[k, 0:height, :] = q if c == 0 else sums[k, 0:height, :] + q
-        grouped(lv.pairs, group, plane)
+    own = pl.ds(lv.own_at, height)
+    ghost_planes(u[1], u[0], lv)
+    mask = lv.odd(height, 0)
+
+    def plane(k):
+        s, v = gather_sum(u[0], u[1], hb[0], lv.zo + k, lv.yo, height, mask, lv.m[own, :])
+        sums[lv.z_at + k, own, :] = sums[lv.z_at + k, own, :] + (s - 6.0 * v)
+    grouped(lv.pairs, TILE if lv.pairs % TILE == 0 else 6, plane)
 
     half = lv.lanes // 2
     rows = TILE * (-(-(lv.rows // 2) // TILE))
@@ -199,8 +217,8 @@
     def fold(pair):
         c = []
         for s in range(2):
-            z = 2 * pair + s
-            v = sums[z, pl.ds(0, rows, stride=2), :] + sums[z, pl.ds(1, rows, stride=2), :]
+            z = lv.z_at + 2 * pair + s
+            v = sums[z, pl.ds(lv.own_at, rows, stride=2), :] + sums[z, pl.ds(lv.own_at + 1, rows, stride=2), :]
             v = pick(v, even_idx) + pick(v, odd_idx)
             c.append(flat(tiled(v) * scale))
         coarse[0][zc + pair, pl.ds(yc, rows), :] = choose(mask, c[1], c[0])
@@ -281,7 +299,7 @@
 def kernel(f_hbm, u_hbm, out_hbm, *scratch):
     (u0r, u0b, f0r, f0b, u1r, u1b, h1r, h1b, u2r, u2b, h2r, h2b, u3r, u3b, h3r, h3b, u4r, u4b, h4r, h4b,
      u5r, u5b, h5r, h5b, d0, d1, d2, d3, d4, cx0, cx1, cx2, cx3, cx4, t0, t1, t2, t3, t4,
-     m0, m1, m2, m3, m4, m5, raw, xs, xr0, xr1, xs1, xr2, c2r, c2b, box, gbox,
+     m0, m1, m2, m3, m4, m5, raw, xs, xr0, xr1, xs1, xr2, ys, yr, zs, zr, es, er, c2r, c2b, box, gbox,
      in_sem, out_sem, x_send, x_recv, send, recv, g_send, g_recv) = scratch
     zi, yi, xi = lax.axis_index('z'), lax.axis_index('y'), lax.axis_index('x')
     peers = ({'x': 1 - xi}, {'y': 1 - yi}, {'z': 1 - zi}, {'z': 1 - zi, 'y': 1 - yi})
@@ -294,19 +312,14 @@
     for n in range(SLOTS):
         load(n).start()
 
-    for ref in (u0r, u0b, f0r, f0b, d0):
+    for ref in (u0r, u0b, f0r, f0b):
         def clear(i, ref=ref):
             ref[i] = jnp.zeros((NY[0], WIDTH), F32)
         loop(NZ[0], clear)
-    for ref in (h1r.at[0], h1b.at[0], h1r.at[1], h1b.at[1], u1r, u1b, d1):
+    for ref in (h1r.at[0], h1b.at[0], h1r.at[1], h1b.at[1]):
         def clear(i, ref=ref):
             ref[i] = jnp.zeros((NY[1], WIDTH), F32)
         loop(NZ[1], clear)
-    for ref in (u2r, u2b, h2r, h2b, u3r, u3b, h3r, h3b, u4r, u4b, h4r, h4b, u5r, u5b, h5r, h5b, d2, d3, d4,
-                cx0, cx1, cx2, cx3, cx4, t0, t1, t2, t3, t4, box):
-        def clear(i, ref=ref):
-            ref[i] = jnp.zeros(ref.shape[1:], F32)
-        loop(ref.shape[0], clear)
 
     barrier = pltpu.get_barrier_semaphore()
     for peer in peers:
@@ -403,6 +416,43 @@
                     copy.start()
                 copies.append(copy)
         return copies
+
+    class Faces:
+        def __init__(self, h, lv, cycle):
+            self.h, self.cycle = h, cycle
+            thick = DEEP // 2
+            y_in, z_in = lv.yo + (lv.rows - DEEP) * (1 - yi), lv.zo + (lv.pairs - thick) * (1 - zi)
+            y_to, z_to = lv.yo + lv.rows - (lv.rows + DEEP) * yi, lv.zo + lv.pairs - (lv.pairs + thick) * zi
+            self.parts = ((ys, yr, lv.zo, lv.pairs, y_in, DEEP, lv.zo, y_to),
+                          (zs, zr, z_in, thick, lv.yo, lv.rows, z_to, lv.yo),
+                          (es, er, z_in, thick, y_in, DEEP, z_to, y_to))
+            self.copies = []
+            for n, (out, into, z, planes, y, rows, _, _) in enumerate(self.parts):
+                lane = lax.broadcasted_iota(jnp.int32, (rows, WIDTH), 1)
+
+                def pack(i):
+                    r, b = h[0][z + i, pl.ds(y, rows), :], h[1][z + i, pl.ds(y, rows), :]
+                    out[i] = jnp.where(lane < 64, turn(r, XHALO * xi), turn(b, XHALO * xi + 64))
+                grouped(planes, 6, pack)
+                at = 12 + n
+                copy = pltpu.make_async_remote_copy(
+                    src_ref=out, dst_ref=into.at[cycle], send_sem=send.at[at], recv_sem=recv.at[at],
+                    device_id=peers[n + 1], device_id_type=MESH)
+                copy.start()
+                self.copies.append(copy)
+
+        def finish(self):
+            for copy, (_, into, _, planes, _, rows, z, y) in zip(self.copies, self.parts):
+                copy.wait()
+                lane = lax.broadcasted_iota(jnp.int32, (rows, WIDTH), 1)
+                valid = jnp.logical_or(lane < 64 - XHALO * xi, lane >= WIDTH - XHALO * xi)
+
+                def unpack(i):
+                    v = into[self.cycle, i]
+                    for c in range(2):
+                        w = turn(v, lax.rem(WIDTH - 64 * c - XHALO * xi, WIDTH))
+                        self.h[c][z + i, pl.ds(y, rows), :] = jnp.where(valid, w, 0.0)
+                grouped(planes, 6, unpack)
 
     def gather_level2(cycle):
         def pack_box(i):
@@ -456,6 +506,11 @@
     faces = send_faces(((u0r, 2, 4), (u0b, 3, 5)), l0, 0)
     x_f.finish()
     faces += send_faces(((f0r, 2, 4), (f0b, 2, 4)), l0, 6)
+    for ref in (u1r, u1b, u2r, u2b, h2r, h2b, u3r, u3b, h3r, h3b, u4r, u4b, h4r, h4b, u5r, u5b, h5r, h5b,
+                d0, d1, d2, d3, d4, cx0, cx1, cx2, cx3, cx4, t0, t1, t2, t3, t4):
+        def clear(i, ref=ref):
+            ref[i] = jnp.zeros(ref.shape[1:], F32)
+        loop(ref.shape[0], clear)
     for copy in faces:
         copy.wait()
 
@@ -463,18 +518,21 @@
         h1 = (h1r.at[cycle], h1b.at[cycle])
         hs = ((f0r, f0b), h1, (h2r, h2b), (h3r, h3b), (h4r, h4b), (h5r, h5b))
         l1 = lvs[1]
-        loop(2, lambda i: sweep(us[0], hs[0], l0))
+        sweep(us[0], hs[0], l0)
+        relax(us[0], hs[0], l0, 0)
+        relax(us[0], hs[0], l0, 1, ts[0])
         restrict(us[0], hs[0], l0, ts[0], h1, (ZO[1], YO[1]))
         Columns(h1, l1, xs1, xr2.at[cycle], TILE).finish()
-        faces = send_faces(((h1[0], 6, 12), (h1[1], 6, 12)), l1, 12)
+        faces = Faces(h1, l1, cycle)
         Columns(us[0], l0, xs, xr1.at[cycle], 4).finish()
-        for copy in faces:
-            copy.wait()
+        faces.finish()
         for level in range(1, 5):
             lv = lvs[level]
             zero_start(us[level], hs[level], lv)
-            half_sweep(us[level][1], us[level][0], hs[level][1], lv, 1)
-            sweep(us[level], hs[level], lv)
+            u, h = us[level], hs[level]
+            relax(u, h, lv, 1)
+            relax(u, h, lv, 0)
+            relax(u, h, lv, 1, ts[level])
             if level == 1:
                 restrict(us[1], h1, l1, ts[1], (c2r, c2b), (0, 0))
                 gather_level2(cycle)
@@ -487,7 +545,7 @@
                 restrict(us[level], hs[level], lv, ts[level], hs[level + 1], (ZO[level + 1], YO[level + 1]))
         lv = lvs[5]
         zero_start(us[5], hs[5], lv)
-        half_sweep(us[5][1], us[5][0], hs[5][1], lv, 1)
+        relax(us[5], hs[5], lv, 1)
         loop(COARSE_SWEEPS - 1, lambda i: sweep(us[5], hs[5], lvs[5]))
         for level in range(4, -1, -1):
             lv = lvs[level]
@@ -532,12 +590,16 @@
     for level in range(2, 6):
         shapes += [arr[level]] * 4
     shapes += arr[:5]
-    shapes += [vmem(56, 80, WIDTH), vmem(30, 48, WIDTH), vmem(BOX, 40, WIDTH), vmem(12, 32, WIDTH), vmem(6, BOX, WIDTH)]
-    shapes += [vmem(48, BRICK, WIDTH), vmem(BOX, 48, WIDTH), vmem(BOX, 48, WIDTH), vmem(12, 32, WIDTH), vmem(6, XHALO, WIDTH)]
+    for extra in (BOX, 0):
+        for level in range(5):
+            rows = WINDOW[level] // 2 + extra if extra else -(-WINDOW[level] // XHALO) * XHALO
+            shapes.append(vmem(PAIRS[level] + ZHALO[level], rows, WIDTH))
     shapes += [vmem(height, WIDTH) for height in WINDOW]
     shapes += [vmem(SLOTS, CHUNK, BRICK, BRICK)]
     shapes += [vmem(4, 6, BRICK, WIDTH), vmem(4, 6, BRICK, WIDTH), vmem(2, 2, 6, BRICK, WIDTH)]
     shapes += [vmem(2, 3, 48, WIDTH), vmem(2, 2, 3, 48, WIDTH)]
+    for planes, rows in ((BOX, DEEP), (DEEP // 2, ROWS[1]), (DEEP // 2, DEEP)):
+        shapes += [vmem(planes, rows, WIDTH), vmem(2, planes, rows, WIDTH)]
     shapes += [vmem(12, BOX, WIDTH), vmem(12, BOX, WIDTH), vmem(2, 2, 3, BOX, WIDTH), vmem(2, TILE, 2, 3, BOX, WIDTH)]
     dma = pltpu.SemaphoreType.DMA
     shapes += [dma((SLOTS,)), dma((SLOTS,)), dma((10,)), dma((10,)), dma((BOX,)), dma((BOX,)), dma((2, 7)), dma((2, 7))]

time: 184 us -> 168 us (0.913)
  Pallas kernels: 179 us -> 163 us
    pallas_call x1, Pallas kernels: 179 us -> 163 us  [local_solve(): pl.pallas_call(kernel, out_shape=jax.ShapeDtypeStruct(source.shape, F32),...]
where the time goes in v3:
time: 168 us; the launch traced here: 167 us
  Pallas kernels  163 us (97%)
  local copies, waits for them, and re-layouts  4.84 us (3%)
    pallas_call x1, Pallas kernels, local_solve(): pl.pallas_call(kernel, out_shape=jax.ShapeDtypeStruct(source.shape, F32),...  163 us
    unnamed x1, local copies, waits for them, and re-layouts  4.84 us

profile of v3, /device:TPU:0, one launch (start us, length us, event | category | flops | bytes accessed | tf_op | source)
XLA Modules:
  0.0 167.4 jit_solution(10551078010010401741)
XLA Ops:
  0.0 162.5 %multigrid.1 = f32[96,96,96]{2,1,0:T(8,128)} custom-call(f32[96,96,96]{2,1,0:T(8,128)} %f_hbm.1, f32[96,96,96]{2,1,0:T(8,128)} %u_hbm.1), custom_call_target="tpu_custom_call" | custom-call | tf_op jit(solution)/shard_map/multigrid/pallas_call | solution.py:613
  162.5 4.8 %copy.4 = f32[96,96,96]{2,1,0:T(8,128)} copy(f32[96,96,96]{2,1,0:T(8,128)} %multigrid.1) | data formatting | bytes 7077888

commit v4 on v3

--- a/solution.py
+++ b/solution.py
@@ -11,17 +11,16 @@
 F32 = jnp.float32
 MESH = pl.DeviceIdType.MESH
 
-PAIRS = (48, 24, 24, 12, 6, 3)
-ROWS = (96, 48, 48, 24, 12, 6)
-LANES = (96, 48, 48, 24, 12, 6)
+ROWS = LANES = (96, 48, 48, 24, 12, 6)
+PAIRS = tuple(rows // 2 for rows in ROWS)
 ZO = (9, 7, 1, 1, 1, 1)
-NZ = (66, 38, 26, 14, 8, 5)
+NZ = tuple(pairs + 2 * first for pairs, first in zip(PAIRS, ZO))
 YO = (24, 24, 8, 8, 8, 8)
-NY = (144, 96, 64, 40, 32, 24)
+NY = tuple(-(-rows // 8) * 8 + 2 * first for rows, first in zip(ROWS, YO))
 ZHALO = (8, 6, 0, 0, 0, 0)
 YHALO = (16, 16, 0, 0, 0, 0)
-WINDOW = (112, 64, 48, 24, 16, 8)
-UNROLL = (8, 10, 12, 12, 6, 3)
+WINDOW = tuple(-(-(rows + halo) // 8) * 8 for rows, halo in zip(ROWS, YHALO))
+UNROLL = (14, 15, 24, 12, 6, 3)
 CHUNK = 16
 SLOTS = 4
 WIDTH = 128
@@ -30,6 +29,7 @@
 BOX = 24
 XHALO = 16
 DEEP = 12
+HALF = 64
 
 
 def iotas(shape=(TILE, WIDTH)):
@@ -37,18 +37,19 @@
 
 
 class Level:
-    def __init__(self, level, zi, yi, xi, m):
+    def __init__(self, level, zi, yi, xi, m, zhalo, yhalo, unroll):
         self.level = level
+        self.unroll = unroll
         self.split = level < 2
         self.pairs, self.rows, self.lanes = PAIRS[level], ROWS[level], LANES[level]
         self.zo, self.yo = ZO[level], YO[level]
-        self.planes = self.pairs + ZHALO[level]
-        self.height = WINDOW[level]
+        self.planes = self.pairs + zhalo
+        self.height = TILE * (-(-(self.rows + yhalo) // TILE))
         self.own_height = TILE * (-(-self.rows // TILE))
         if self.split:
-            self.zs = self.zo - ZHALO[level] * zi
-            self.ys = pl.multiple_of(self.yo - YHALO[level] * yi, TILE)
-            self.own_at = pl.multiple_of(YHALO[level] * yi, TILE)
+            self.zs = self.zo - zhalo * zi
+            self.ys = pl.multiple_of(self.yo - yhalo * yi, TILE)
+            self.own_at = pl.multiple_of(yhalo * yi, TILE)
         else:
             self.zs, self.ys, self.own_at = self.zo, self.yo, 0
         self.zi = zi
@@ -163,10 +164,12 @@
         m = lv.m[...]
         s, old = gather_sum(a, b, hb, z, lv.ys, lv.height, mask, m)
         new = lv.scaled(s)
+        if sums is not None:
+            new = new + lv.scaled(s - 6.0 * new)
         a[z, lv.row, :] = new
         if sums is not None:
             sums[k, 0:lv.height, :] = m * (old - new)
-    grouped(lv.planes, UNROLL[lv.level], plane)
+    grouped(lv.planes, lv.unroll, plane)
     if sums is not None:
         for n, (to, frm) in enumerate(lv.ghosts()):
             delta = -(a[frm, lv.row, :] + b[to, lv.row, :])
@@ -191,7 +194,7 @@
 
     def plane(k):
         u[0][lv.zs + k, lv.row, :] = lv.scaled(hb[0][lv.zs + k, lv.row, :])
-    grouped(lv.planes, UNROLL[lv.level], plane)
+    grouped(lv.planes, lv.unroll, plane)
 
 
 def restrict(u, hb, lv, sums, coarse, coarse_at):
@@ -203,7 +206,7 @@
     def plane(k):
         s, v = gather_sum(u[0], u[1], hb[0], lv.zo + k, lv.yo, height, mask, lv.m[own, :])
         sums[lv.z_at + k, own, :] = sums[lv.z_at + k, own, :] + (s - 6.0 * v)
-    grouped(lv.pairs, TILE if lv.pairs % TILE == 0 else 6, plane)
+    grouped(lv.pairs, min(12, lv.pairs), plane)
 
     half = lv.lanes // 2
     rows = TILE * (-(-(lv.rows // 2) // TILE))
@@ -296,13 +299,62 @@
     grouped(planes, 2, along_z)
 
 
+def coarsest(h, u, lv, qu, qh):
+    edge = lv.lanes
+    box = (edge, TILE, WIDTH)
+    x, y, lane = (lax.broadcasted_iota(jnp.int32, box, d) for d in range(3))
+    rows = pl.ds(TILE, TILE)
+    for c in range(2):
+        for k in range(lv.pairs):
+            v = h[c][lv.zo + k, rows, :]
+            for i in range(edge):
+                qh[c, k, i] = pick(v, jnp.full((TILE, WIDTH), i, jnp.int32))
+    clear_all((qu,))
+    inner = ones(y < edge).astype(F32) / 6.0
+    faces = (ones(x == 0) + ones(x == edge - 1) + ones(y == 0) + ones(y == edge - 1)).astype(F32)
+    own = pl.ds(1, edge)
+
+    def sweeps(_):
+        for c in range(2):
+            up = lax.rem(x + y + c, 2) == 1
+            up_f = ones(up).astype(F32)
+            for k in range(lv.pairs):
+                m = faces
+                if k == 0:
+                    m = m + (1.0 - up_f)
+                if k == lv.pairs - 1:
+                    m = m + up_f
+                z = k + 1
+                b, a = qu.at[1 - c], qu.at[c]
+                s = b[z, own, rows, :] + jnp.where(up, b[z + 1, own, rows, :], b[z - 1, own, rows, :])
+                s = s + (b[z, own, pl.ds(TILE - 1, TILE), :] + b[z, own, pl.ds(TILE + 1, TILE), :])
+                s = s + (b[z, pl.ds(0, edge), rows, :] + b[z, pl.ds(2, edge), rows, :])
+                a[z, own, rows, :] = (s + (qh[c, k] - m * a[z, own, rows, :])) * inner
+    loop(COARSE_SWEEPS, sweeps)
+    for c in range(2):
+        for k in range(lv.pairs):
+            v = qu[c, k + 1, own, rows, :]
+            total = jnp.where(lane[0] == 0, v[0], 0.0)
+            for i in range(1, edge):
+                total = jnp.where(lane[0] == i, v[i], total)
+            u[c][lv.zo + k, rows, :] = total
+
+
+def clear_all(refs):
+    for ref in refs:
+        def clear(i, ref=ref):
+            ref[i] = jnp.zeros(ref.shape[1:], F32)
+        loop(ref.shape[0], clear)
+
+
 def kernel(f_hbm, u_hbm, out_hbm, *scratch):
     (u0r, u0b, f0r, f0b, u1r, u1b, h1r, h1b, u2r, u2b, h2r, h2b, u3r, u3b, h3r, h3b, u4r, u4b, h4r, h4b,
      u5r, u5b, h5r, h5b, d0, d1, d2, d3, d4, cx0, cx1, cx2, cx3, cx4, t0, t1, t2, t3, t4,
-     m0, m1, m2, m3, m4, m5, raw, xs, xr0, xr1, xs1, xr2, ys, yr, zs, zr, es, er, c2r, c2b, box, gbox,
+     m0, m1, m2, m3, m4, m5, m6, raw, xs, xr0, xr1, xs1, xr2, ys, yr, zs, zr, es, er, qu, qh, c2r, c2b, box, gbox,
      in_sem, out_sem, x_send, x_recv, send, recv, g_send, g_recv) = scratch
     zi, yi, xi = lax.axis_index('z'), lax.axis_index('y'), lax.axis_index('x')
-    peers = ({'x': 1 - xi}, {'y': 1 - yi}, {'z': 1 - zi}, {'z': 1 - zi, 'y': 1 - yi})
+    nx, ny, nz = 1 - xi, 1 - yi, 1 - zi
+    peers = ({'x': nx}, {'y': ny}, {'z': nz}, {'z': nz, 'y': ny})
 
     chunks = [(src, c) for src in (u_hbm, f_hbm) for c in range(BRICK // CHUNK)]
 
@@ -313,13 +365,9 @@
         load(n).start()
 
     for ref in (u0r, u0b, f0r, f0b):
-        def clear(i, ref=ref):
-            ref[i] = jnp.zeros((NY[0], WIDTH), F32)
-        loop(NZ[0], clear)
+        clear_all((ref,))
     for ref in (h1r.at[0], h1b.at[0], h1r.at[1], h1b.at[1]):
-        def clear(i, ref=ref):
-            ref[i] = jnp.zeros((NY[1], WIDTH), F32)
-        loop(NZ[1], clear)
+        clear_all((ref,))
 
     barrier = pltpu.get_barrier_semaphore()
     for peer in peers:
@@ -347,7 +395,9 @@
             load(n + SLOTS).start()
     pl.semaphore_wait(barrier, len(peers))
 
-    lvs = [Level(level, zi, yi, xi, m) for level, m in enumerate((m0, m1, m2, m3, m4, m5))]
+    lvs = [Level(level, zi, yi, xi, m, ZHALO[level], YHALO[level], UNROLL[level])
+           for level, m in enumerate((m0, m1, m2, m3, m4, m5))]
+    near = Level(0, zi, yi, xi, m6, 4, TILE, 13)
     us = ((u0r, u0b), (u1r, u1b), (u2r, u2b), (u3r, u3b), (u4r, u4b), (u5r, u5b))
     ds_ = (d0, d1, d2, d3, d4)
     cxs = (cx0, cx1, cx2, cx3, cx4)
@@ -362,7 +412,7 @@
             self.wide = lax.broadcasted_iota(jnp.int32, (lv.rows, WIDTH), 1)
             self.row = pl.ds(lv.yo, lv.rows)
             group = lax.div(self.wide, XHALO)
-            from_lane = (lv.lanes - XHALO) * (1 - xi)
+            from_lane = (lv.lanes - XHALO) * nx
             self.copies = []
             for n, a in enumerate(arrays):
                 def pack_x(i, a=a, n=n):
@@ -398,9 +448,9 @@
         copies = []
         for a, zn, yn in specs:
             z_own, y_own = pl.ds(lv.zo, lv.pairs), pl.ds(lv.yo, lv.rows)
-            y_in = lv.yo + (lv.rows - yn) * (1 - yi)
+            y_in = lv.yo + (lv.rows - yn) * ny
             y_to = lv.yo - yn + (lv.rows + yn) * yi
-            z_in = lv.zo + (lv.pairs - zn) * (1 - zi)
+            z_in = lv.zo + (lv.pairs - zn) * nz
             z_to = lv.zo - zn + (lv.pairs + zn) * zi
             parts = (
                 ((z_own, pl.ds(y_in, yn)), (z_own, pl.ds(y_to, yn)), peers[1]),
@@ -421,7 +471,7 @@
         def __init__(self, h, lv, cycle):
             self.h, self.cycle = h, cycle
             thick = DEEP // 2
-            y_in, z_in = lv.yo + (lv.rows - DEEP) * (1 - yi), lv.zo + (lv.pairs - thick) * (1 - zi)
+            y_in, z_in = lv.yo + (lv.rows - DEEP) * ny, lv.zo + (lv.pairs - thick) * nz
             y_to, z_to = lv.yo + lv.rows - (lv.rows + DEEP) * yi, lv.zo + lv.pairs - (lv.pairs + thick) * zi
             self.parts = ((ys, yr, lv.zo, lv.pairs, y_in, DEEP, lv.zo, y_to),
                           (zs, zr, z_in, thick, lv.yo, lv.rows, z_to, lv.yo),
@@ -432,7 +482,7 @@
 
                 def pack(i):
                     r, b = h[0][z + i, pl.ds(y, rows), :], h[1][z + i, pl.ds(y, rows), :]
-                    out[i] = jnp.where(lane < 64, turn(r, XHALO * xi), turn(b, XHALO * xi + 64))
+                    out[i] = jnp.where(lane < HALF, turn(r, XHALO * xi), turn(b, XHALO * xi + HALF))
                 grouped(planes, 6, pack)
                 at = 12 + n
                 copy = pltpu.make_async_remote_copy(
@@ -445,12 +495,12 @@
             for copy, (_, into, _, planes, _, rows, z, y) in zip(self.copies, self.parts):
                 copy.wait()
                 lane = lax.broadcasted_iota(jnp.int32, (rows, WIDTH), 1)
-                valid = jnp.logical_or(lane < 64 - XHALO * xi, lane >= WIDTH - XHALO * xi)
+                valid = jnp.logical_or(lane < HALF - XHALO * xi, lane >= WIDTH - XHALO * xi)
 
                 def unpack(i):
                     v = into[self.cycle, i]
                     for c in range(2):
-                        w = turn(v, lax.rem(WIDTH - 64 * c - XHALO * xi, WIDTH))
+                        w = turn(v, lax.rem(WIDTH - HALF * c - XHALO * xi, WIDTH))
                         self.h[c][z + i, pl.ds(y, rows), :] = jnp.where(valid, w, 0.0)
                 grouped(planes, 6, unpack)
 
@@ -470,7 +520,8 @@
                 device_id=peer, device_id_type=MESH)
             copy.start()
             copies.append(copy)
-        for n, (dz, dy) in ((1, (0, 1)), (2, (1, 0)), (3, (1, 1))):
+        for n in range(1, len(peers)):
+            dz, dy = divmod(n, 2)
             copies[n].wait_recv()
             sz, sy = zi + dz - 2 * dz * zi, yi + dy - 2 * dy * yi
             at = 4 * xi + 2 * sz + sy
@@ -505,12 +556,11 @@
     x_u.finish()
     faces = send_faces(((u0r, 2, 4), (u0b, 3, 5)), l0, 0)
     x_f.finish()
-    faces += send_faces(((f0r, 2, 4), (f0b, 2, 4)), l0, 6)
+    faces += send_faces(((f0r, 2, 4),), l0, 6)
+    send_faces(((f0b, 2, 3),), l0, 9)
     for ref in (u1r, u1b, u2r, u2b, h2r, h2b, u3r, u3b, h3r, h3b, u4r, u4b, h4r, h4b, u5r, u5b, h5r, h5b,
                 d0, d1, d2, d3, d4, cx0, cx1, cx2, cx3, cx4, t0, t1, t2, t3, t4):
-        def clear(i, ref=ref):
-            ref[i] = jnp.zeros(ref.shape[1:], F32)
-        loop(ref.shape[0], clear)
+        clear_all((ref,))
     for copy in faces:
         copy.wait()
 
@@ -518,10 +568,16 @@
         h1 = (h1r.at[cycle], h1b.at[cycle])
         hs = ((f0r, f0b), h1, (h2r, h2b), (h3r, h3b), (h4r, h4b), (h5r, h5b))
         l1 = lvs[1]
-        sweep(us[0], hs[0], l0)
-        relax(us[0], hs[0], l0, 0)
-        relax(us[0], hs[0], l0, 1, ts[0])
-        restrict(us[0], hs[0], l0, ts[0], h1, (ZO[1], YO[1]))
+        relax(us[0], (f0r, f0b), near, 0)
+
+        @pl.when(cycle == 0)
+        def black_source_arrived():
+            for copy in send_faces(((f0b, 2, 3),), l0, 9, False):
+                copy.wait()
+        relax(us[0], (f0r, f0b), near, 1)
+        relax(us[0], (f0r, f0b), near, 0)
+        relax(us[0], (f0r, f0b), near, 1, ts[0])
+        restrict(us[0], (f0r, f0b), near, ts[0], h1, (ZO[1], YO[1]))
         Columns(h1, l1, xs1, xr2.at[cycle], TILE).finish()
         faces = Faces(h1, l1, cycle)
         Columns(us[0], l0, xs, xr1.at[cycle], 4).finish()
@@ -543,10 +599,7 @@
                     send_faces(((f0r, 4, TILE), (f0b, 4, TILE)), l0, 0)
             else:
                 restrict(us[level], hs[level], lv, ts[level], hs[level + 1], (ZO[level + 1], YO[level + 1]))
-        lv = lvs[5]
-        zero_start(us[5], hs[5], lv)
-        relax(us[5], hs[5], lv, 1)
-        loop(COARSE_SWEEPS - 1, lambda i: sweep(us[5], hs[5], lvs[5]))
+        coarsest(hs[5], us[5], lvs[5], qu, qh)
         for level in range(4, -1, -1):
             lv = lvs[level]
             if level == 0:
@@ -558,7 +611,16 @@
                     for copy in send_faces(((f0r, 4, TILE), (f0b, 4, TILE)), l0, 0, False):
                         copy.wait()
             prolong(us[level], us[level + 1], lv, lvs[level + 1], yi, xi, cxs[level], ds_[level])
-            loop(2, lambda i, lv=lv, level=level: sweep(us[level], hs[level], lv))
+            if level:
+                loop(2, lambda i, lv=lv, level=level: sweep(us[level], hs[level], lv))
+
+        @pl.when(cycle < CYCLES - 1)
+        def wide_sweeps():
+            loop(2, lambda i: sweep(us[0], (f0r, f0b), l0))
+
+        @pl.when(cycle == CYCLES - 1)
+        def last_sweeps():
+            loop(2, lambda i: sweep(us[0], (f0r, f0b), near))
     loop(CYCLES, v_cycle)
 
     stores = []
@@ -594,12 +656,14 @@
         for level in range(5):
             rows = WINDOW[level] // 2 + extra if extra else -(-WINDOW[level] // XHALO) * XHALO
             shapes.append(vmem(PAIRS[level] + ZHALO[level], rows, WIDTH))
-    shapes += [vmem(height, WIDTH) for height in WINDOW]
+    shapes += [vmem(height, WIDTH) for height in (*WINDOW, WINDOW[0] - TILE)]
     shapes += [vmem(SLOTS, CHUNK, BRICK, BRICK)]
     shapes += [vmem(4, 6, BRICK, WIDTH), vmem(4, 6, BRICK, WIDTH), vmem(2, 2, 6, BRICK, WIDTH)]
     shapes += [vmem(2, 3, 48, WIDTH), vmem(2, 2, 3, 48, WIDTH)]
     for planes, rows in ((BOX, DEEP), (DEEP // 2, ROWS[1]), (DEEP // 2, DEEP)):
         shapes += [vmem(planes, rows, WIDTH), vmem(2, planes, rows, WIDTH)]
+    last = LANES[5]
+    shapes += [vmem(2, PAIRS[5] + 2, last + 2, 3 * TILE, WIDTH), vmem(2, PAIRS[5], last, TILE, WIDTH)]
     shapes += [vmem(12, BOX, WIDTH), vmem(12, BOX, WIDTH), vmem(2, 2, 3, BOX, WIDTH), vmem(2, TILE, 2, 3, BOX, WIDTH)]
     dma = pltpu.SemaphoreType.DMA
     shapes += [dma((SLOTS,)), dma((SLOTS,)), dma((10,)), dma((10,)), dma((BOX,)), dma((BOX,)), dma((2, 7)), dma((2, 7))]

time: 168 us -> 156 us (0.929)
  Pallas kernels: 163 us -> 151 us
    pallas_call x1, Pallas kernels: 163 us -> 151 us  [local_solve(): pl.pallas_call(kernel, out_shape=jax.ShapeDtypeStruct(source.shape, F32),...]
where the time goes in v4:
time: 156 us
  Pallas kernels  151 us (97%)
  local copies, waits for them, and re-layouts  4.84 us (3%)
    pallas_call x1, Pallas kernels, local_solve(): pl.pallas_call(kernel, out_shape=jax.ShapeDtypeStruct(source.shape, F32),...  151 us
    unnamed x1, local copies, waits for them, and re-layouts  4.84 us

profile of v4, /device:TPU:0, one launch (start us, length us, event | category | flops | bytes accessed | tf_op | source)
XLA Modules:
  0.0 155.8 jit_solution(5204336439041803291)
XLA Ops:
  0.0 150.9 %multigrid.1 = f32[96,96,96]{2,1,0:T(8,128)} custom-call(f32[96,96,96]{2,1,0:T(8,128)} %f_hbm.1, f32[96,96,96]{2,1,0:T(8,128)} %u_hbm.1), custom_call_target="tpu_custom_call" | custom-call | tf_op jit(solution)/shard_map/multigrid/pallas_call | solution.py:677
  150.9 4.8 %copy.4 = f32[96,96,96]{2,1,0:T(8,128)} copy(f32[96,96,96]{2,1,0:T(8,128)} %multigrid.1) | data formatting | bytes 7077888

commit v5 on v4

--- a/solution.py
+++ b/solution.py
@@ -29,6 +29,7 @@
 BOX = 24
 XHALO = 16
 DEEP = 12
+LAST = 5
 HALF = 64
 
 
@@ -381,16 +382,17 @@
         slot = n % SLOTS
         first = n < len(chunks) // 2
         red, black = (u0r, u0b) if first else (f0r, f0b)
-        start = ZO[0] + (n % (BRICK // CHUNK)) * (CHUNK // 2)
+        half = CHUNK // 2
+        start = ZO[0] + (n % (BRICK // CHUNK)) * half
 
         def pack(i):
             p0, p1 = raw[slot, 2 * i], raw[slot, 2 * i + 1]
             r, b = jnp.where(odd96, p1, p0), jnp.where(odd96, p0, p1)
             if not first:
                 r, b = r * h_sq, b * h_sq
-            red[start + i, YO[0]:YO[0] + BRICK, 0:BRICK] = r
-            black[start + i, YO[0]:YO[0] + BRICK, 0:BRICK] = b
-        loop(CHUNK // 2, pack)
+            red[start + i, YO[0]:YO[0] + BRICK, :BRICK] = r
+            black[start + i, YO[0]:YO[0] + BRICK, :BRICK] = b
+        loop(half, pack)
         if n + SLOTS < len(chunks):
             load(n + SLOTS).start()
     pl.semaphore_wait(barrier, len(peers))
@@ -446,16 +448,21 @@
 
     def send_faces(specs, lv, sem_at, start=True):
         copies = []
-        for a, zn, yn in specs:
+        def layers(first, count, size, skip, high):
+            inside = first + skip + (count - size - 2 * skip) * (1 - high)
+            outside = first - skip - size + (count + size + 2 * skip) * high
+            return pl.ds(inside, size), pl.ds(outside, size)
+
+        for a, zn, yn, *there in specs:
+            z_skip, y_skip = there or (0, 0)
             z_own, y_own = pl.ds(lv.zo, lv.pairs), pl.ds(lv.yo, lv.rows)
-            y_in = lv.yo + (lv.rows - yn) * ny
-            y_to = lv.yo - yn + (lv.rows + yn) * yi
-            z_in = lv.zo + (lv.pairs - zn) * nz
-            z_to = lv.zo - zn + (lv.pairs + zn) * zi
+            y_in, y_to = layers(lv.yo, lv.rows, yn - y_skip, y_skip, yi)
+            z_in, z_to = layers(lv.zo, lv.pairs, zn - z_skip, z_skip, zi)
+            y_all, z_all = layers(lv.yo, lv.rows, yn, 0, yi), layers(lv.zo, lv.pairs, zn, 0, zi)
             parts = (
-                ((z_own, pl.ds(y_in, yn)), (z_own, pl.ds(y_to, yn)), peers[1]),
-                ((pl.ds(z_in, zn), y_own), (pl.ds(z_to, zn), y_own), peers[2]),
-                ((pl.ds(z_in, zn), pl.ds(y_in, yn)), (pl.ds(z_to, zn), pl.ds(y_to, yn)), peers[3]),
+                ((z_own, y_in), (z_own, y_to), peers[1]),
+                ((z_in, y_own), (z_to, y_own), peers[2]),
+                ((z_all[0], y_all[0]), (z_all[1], y_all[1]), peers[3]),
             )
             for src, dst, peer in parts:
                 at = sem_at + len(copies)
@@ -481,7 +488,7 @@
                 lane = lax.broadcasted_iota(jnp.int32, (rows, WIDTH), 1)
 
                 def pack(i):
-                    r, b = h[0][z + i, pl.ds(y, rows), :], h[1][z + i, pl.ds(y, rows), :]
+                    r, b = (colour[z + i, pl.ds(y, rows), :] for colour in h)
                     out[i] = jnp.where(lane < HALF, turn(r, XHALO * xi), turn(b, XHALO * xi + HALF))
                 grouped(planes, 6, pack)
                 at = 12 + n
@@ -564,6 +571,8 @@
     for copy in faces:
         copy.wait()
 
+    deeper = ((f0r, 4, TILE, 2, 4), (f0b, 4, TILE, 2, 3))
+
     def v_cycle(cycle):
         h1 = (h1r.at[cycle], h1b.at[cycle])
         hs = ((f0r, f0b), h1, (h2r, h2b), (h3r, h3b), (h4r, h4b), (h5r, h5b))
@@ -582,7 +591,11 @@
         faces = Faces(h1, l1, cycle)
         Columns(us[0], l0, xs, xr1.at[cycle], 4).finish()
         faces.finish()
-        for level in range(1, 5):
+
+        @pl.when(cycle == 0)
+        def deeper_source():
+            send_faces(deeper, l0, 0)
+        for level in range(1, LAST):
             lv = lvs[level]
             zero_start(us[level], hs[level], lv)
             u, h = us[level], hs[level]
@@ -590,16 +603,14 @@
             relax(u, h, lv, 0)
             relax(u, h, lv, 1, ts[level])
             if level == 1:
-                restrict(us[1], h1, l1, ts[1], (c2r, c2b), (0, 0))
+                restrict(u, h, lv, ts[level], (c2r, c2b), (0, 0))
                 gather_level2(cycle)
                 pending = send_faces(((u0r, 4, TILE), (u0b, 5, 9)), l0, 18)
 
-                @pl.when(cycle == 0)
-                def deeper_source():
-                    send_faces(((f0r, 4, TILE), (f0b, 4, TILE)), l0, 0)
             else:
-                restrict(us[level], hs[level], lv, ts[level], hs[level + 1], (ZO[level + 1], YO[level + 1]))
-        coarsest(hs[5], us[5], lvs[5], qu, qh)
+                lower = level + 1
+                restrict(u, h, lv, ts[level], hs[lower], (ZO[lower], YO[lower]))
+        coarsest(hs[LAST], us[LAST], lvs[LAST], qu, qh)
         for level in range(4, -1, -1):
             lv = lvs[level]
             if level == 0:
@@ -608,7 +619,7 @@
 
                 @pl.when(cycle == 0)
                 def deeper_source_arrived():
-                    for copy in send_faces(((f0r, 4, TILE), (f0b, 4, TILE)), l0, 0, False):
+                    for copy in send_faces(deeper, l0, 0, False):
                         copy.wait()
             prolong(us[level], us[level + 1], lv, lvs[level + 1], yi, xi, cxs[level], ds_[level])
             if level:
@@ -630,11 +641,11 @@
             stores[n - SLOTS].wait()
 
         def unpack(i):
-            z = ZO[0] + n * (CHUNK // 2) + i
-            r, b = u0r[z, YO[0]:YO[0] + BRICK, 0:BRICK], u0b[z, YO[0]:YO[0] + BRICK, 0:BRICK]
+            z = l0.zo + n * half + i
+            r, b = (colour[z, YO[0]:YO[0] + BRICK, :BRICK] for colour in us[0])
             raw[slot, 2 * i] = jnp.where(odd96, b, r)
             raw[slot, 2 * i + 1] = jnp.where(odd96, r, b)
-        loop(CHUNK // 2, unpack)
+        loop(half, unpack)
         copy = pltpu.make_async_copy(raw.at[slot], out_hbm.at[pl.ds(n * CHUNK, CHUNK)], out_sem.at[slot])
         copy.start()
         stores.append(copy)
@@ -653,7 +664,7 @@
         shapes += [arr[level]] * 4
     shapes += arr[:5]
     for extra in (BOX, 0):
-        for level in range(5):
+        for level in range(LAST):
             rows = WINDOW[level] // 2 + extra if extra else -(-WINDOW[level] // XHALO) * XHALO
             shapes.append(vmem(PAIRS[level] + ZHALO[level], rows, WIDTH))
     shapes += [vmem(height, WIDTH) for height in (*WINDOW, WINDOW[0] - TILE)]
@@ -662,11 +673,12 @@
     shapes += [vmem(2, 3, 48, WIDTH), vmem(2, 2, 3, 48, WIDTH)]
     for planes, rows in ((BOX, DEEP), (DEEP // 2, ROWS[1]), (DEEP // 2, DEEP)):
         shapes += [vmem(planes, rows, WIDTH), vmem(2, planes, rows, WIDTH)]
-    last = LANES[5]
-    shapes += [vmem(2, PAIRS[5] + 2, last + 2, 3 * TILE, WIDTH), vmem(2, PAIRS[5], last, TILE, WIDTH)]
+    last = LANES[LAST]
+    shapes += [vmem(2, PAIRS[LAST] + 2, last + 2, 3 * TILE, WIDTH), vmem(2, PAIRS[LAST], last, TILE, WIDTH)]
     shapes += [vmem(12, BOX, WIDTH), vmem(12, BOX, WIDTH), vmem(2, 2, 3, BOX, WIDTH), vmem(2, TILE, 2, 3, BOX, WIDTH)]
     dma = pltpu.SemaphoreType.DMA
-    shapes += [dma((SLOTS,)), dma((SLOTS,)), dma((10,)), dma((10,)), dma((BOX,)), dma((BOX,)), dma((2, 7)), dma((2, 7))]
+    for shape in ((SLOTS,), (10,), (BOX,), (2, 7)):
+        shapes += [dma(shape), dma(shape)]
     return shapes
 
 

time: 156 us -> 149 us (0.955)
  Pallas kernels: 151 us -> 144 us
    pallas_call x1, Pallas kernels: 151 us -> 144 us  [local_solve(): pl.pallas_call(kernel, out_shape=jax.ShapeDtypeStruct(source.shape, F32),...]
where the time goes in v5:
time: 149 us
  Pallas kernels  144 us (97%)
  local copies, waits for them, and re-layouts  4.84 us (3%)
    pallas_call x1, Pallas kernels, local_solve(): pl.pallas_call(kernel, out_shape=jax.ShapeDtypeStruct(source.shape, F32),...  144 us
    unnamed x1, local copies, waits for them, and re-layouts  4.84 us

profile of v5, /device:TPU:0, one launch (start us, length us, event | category | flops | bytes accessed | tf_op | source)
XLA Modules:
  0.0 148.5 jit_solution(4979475685516720707)
XLA Ops:
  0.0 143.7 %multigrid.1 = f32[96,96,96]{2,1,0:T(8,128)} custom-call(f32[96,96,96]{2,1,0:T(8,128)} %f_hbm.1, f32[96,96,96]{2,1,0:T(8,128)} %u_hbm.1), custom_call_target="tpu_custom_call" | custom-call | tf_op jit(solution)/shard_map/multigrid/pallas_call | solution.py:689
  143.7 4.8 %copy.4 = f32[96,96,96]{2,1,0:T(8,128)} copy(f32[96,96,96]{2,1,0:T(8,128)} %multigrid.1) | data formatting | bytes 7077888

commit v6 on v5

--- a/solution.py
+++ b/solution.py
@@ -377,12 +377,13 @@
     sub, lane = iotas((BRICK, BRICK))
     odd96 = lax.rem(sub + lane, 2) == 1
     h_sq = (1.0 / N) ** 2
-    for n in range(len(chunks)):
+    half = CHUNK // 2
+
+    def ingest(n):
         load(n).wait()
         slot = n % SLOTS
         first = n < len(chunks) // 2
         red, black = (u0r, u0b) if first else (f0r, f0b)
-        half = CHUNK // 2
         start = ZO[0] + (n % (BRICK // CHUNK)) * half
 
         def pack(i):
@@ -395,7 +396,6 @@
         loop(half, pack)
         if n + SLOTS < len(chunks):
             load(n + SLOTS).start()
-    pl.semaphore_wait(barrier, len(peers))
 
     lvs = [Level(level, zi, yi, xi, m, ZHALO[level], YHALO[level], UNROLL[level])
            for level, m in enumerate((m0, m1, m2, m3, m4, m5))]
@@ -558,10 +558,16 @@
         loop(3, unpack_box)
 
     l0 = lvs[0]
-    x_u = Columns((u0r, u0b), l0, xs, xr0, 0)
-    x_f = Columns((f0r, f0b), l0, xs.at[2:4], xr0.at[2:4], 2)
+    count = len(chunks) // 2
+    for n in range(count):
+        ingest(n)
+    pl.semaphore_wait(barrier, len(peers))
+    x_u = Columns(us[0], l0, xs, xr0, 0)
+    for n in range(count):
+        ingest(count + n)
     x_u.finish()
     faces = send_faces(((u0r, 2, 4), (u0b, 3, 5)), l0, 0)
+    x_f = Columns((f0r, f0b), l0, xs.at[2:4], xr0.at[2:4], 2)
     x_f.finish()
     faces += send_faces(((f0r, 2, 4),), l0, 6)
     send_faces(((f0b, 2, 3),), l0, 9)

time: 149 us -> 146 us (0.980)
  Pallas kernels: 144 us -> 141 us
    pallas_call x1, Pallas kernels: 144 us -> 141 us  [local_solve(): pl.pallas_call(kernel, out_shape=jax.ShapeDtypeStruct(source.shape, F32),...]
where the time goes in v6:
time: 146 us
  Pallas kernels  141 us (97%)
  local copies, waits for them, and re-layouts  4.84 us (3%)
    pallas_call x1, Pallas kernels, local_solve(): pl.pallas_call(kernel, out_shape=jax.ShapeDtypeStruct(source.shape, F32),...  141 us
    unnamed x1, local copies, waits for them, and re-layouts  4.84 us

profile of v6, /device:TPU:0, one launch (start us, length us, event | category | flops | bytes accessed | tf_op | source)
XLA Modules:
  0.0 145.6 jit_solution(957717634051615035)
XLA Ops:
  0.0 140.7 %multigrid.1 = f32[96,96,96]{2,1,0:T(8,128)} custom-call(f32[96,96,96]{2,1,0:T(8,128)} %f_hbm.1, f32[96,96,96]{2,1,0:T(8,128)} %u_hbm.1), custom_call_target="tpu_custom_call" | custom-call | tf_op jit(solution)/shard_map/multigrid/pallas_call | solution.py:695
  140.7 4.8 %copy.4 = f32[96,96,96]{2,1,0:T(8,128)} copy(f32[96,96,96]{2,1,0:T(8,128)} %multigrid.1) | data formatting | bytes 7077888

commit v7 on v6

--- a/solution.py
+++ b/solution.py
@@ -189,10 +189,6 @@
 
 
 def zero_start(u, hb, lv):
-    def clear(i):
-        u[1][i] = jnp.zeros(u[1].shape[1:], F32)
-    loop(u[1].shape[0], clear)
-
     def plane(k):
         u[0][lv.zs + k, lv.row, :] = lv.scaled(hb[0][lv.zs + k, lv.row, :])
     grouped(lv.planes, lv.unroll, plane)
@@ -348,7 +344,8 @@
         loop(ref.shape[0], clear)
 
 
-def kernel(f_hbm, u_hbm, out_hbm, *scratch):
+def kernel(f_hbm, u_hbm, *rest):
+    outs, scratch = rest[:2], rest[2:]
     (u0r, u0b, f0r, f0b, u1r, u1b, h1r, h1b, u2r, u2b, h2r, h2b, u3r, u3b, h3r, h3b, u4r, u4b, h4r, h4b,
      u5r, u5b, h5r, h5b, d0, d1, d2, d3, d4, cx0, cx1, cx2, cx3, cx4, t0, t1, t2, t3, t4,
      m0, m1, m2, m3, m4, m5, m6, raw, xs, xr0, xr1, xs1, xr2, ys, yr, zs, zr, es, er, qu, qh, c2r, c2b, box, gbox,
@@ -527,6 +524,7 @@
                 device_id=peer, device_id_type=MESH)
             copy.start()
             copies.append(copy)
+        clear_all((u2b, u3b, u4b))
         for n in range(1, len(peers)):
             dz, dy = divmod(n, 2)
             copies[n].wait_recv()
@@ -596,6 +594,7 @@
         Columns(h1, l1, xs1, xr2.at[cycle], TILE).finish()
         faces = Faces(h1, l1, cycle)
         Columns(us[0], l0, xs, xr1.at[cycle], 4).finish()
+        clear_all((u1b,))
         faces.finish()
 
         @pl.when(cycle == 0)
@@ -641,21 +640,11 @@
     loop(CYCLES, v_cycle)
 
     stores = []
-    for n in range(BRICK // CHUNK):
-        slot = n % SLOTS
-        if n >= SLOTS:
-            stores[n - SLOTS].wait()
-
-        def unpack(i):
-            z = l0.zo + n * half + i
-            r, b = (colour[z, YO[0]:YO[0] + BRICK, :BRICK] for colour in us[0])
-            raw[slot, 2 * i] = jnp.where(odd96, b, r)
-            raw[slot, 2 * i + 1] = jnp.where(odd96, r, b)
-        loop(half, unpack)
-        copy = pltpu.make_async_copy(raw.at[slot], out_hbm.at[pl.ds(n * CHUNK, CHUNK)], out_sem.at[slot])
+    for n, colour in enumerate(us[0]):
+        copy = pltpu.make_async_copy(colour.at[pl.ds(l0.zo, l0.pairs), pl.ds(l0.yo, l0.rows)], outs[n], out_sem.at[n])
         copy.start()
         stores.append(copy)
-    for copy in stores[-SLOTS:]:
+    for copy in stores:
         copy.wait()
 
 
@@ -692,14 +681,18 @@
     spec = P(('batch', 'z'), 'y', 'x')
 
     def local_solve(source, initial_guess):
-        return pl.pallas_call(
+        pairs, rows, lanes = source.shape[0] // 2, source.shape[1], source.shape[2]
+        red, black = pl.pallas_call(
             kernel,
-            out_shape=jax.ShapeDtypeStruct(source.shape, F32),
+            out_shape=[jax.ShapeDtypeStruct((pairs, rows, WIDTH), F32)] * 2,
             in_specs=[pl.BlockSpec(memory_space=pl.ANY)] * 2,
-            out_specs=pl.BlockSpec(memory_space=pl.ANY),
+            out_specs=[pl.BlockSpec(memory_space=pl.ANY)] * 2,
             scratch_shapes=scratch_shapes(),
             compiler_params=pltpu.CompilerParams(collective_id=0, has_side_effects=True, vmem_limit_bytes=67043328),
             name='multigrid',
         )(source, initial_guess)
+        red, black = red[:, None, :, :lanes], black[:, None, :, :lanes]
+        z, y, x = (lax.broadcasted_iota(jnp.int32, (1, 2, rows, lanes), d) for d in range(1, 4))
+        return jnp.where(lax.rem(z + y + x, 2) == 0, red, black).reshape(source.shape)
 
     return jax.shard_map(local_solve, mesh=mesh, in_specs=(spec, spec), out_specs=spec, check_vma=False)

time: 146 us -> 146 us (level)
  other arithmetic: 0 us -> 5.74 us
  local copies, waits for them, and re-layouts: 4.84 us -> 0 us
    select_n x0 -> x1, other arithmetic: none -> 5.1 us  [local_solve(): jnp.where(lax.rem(z + y + x, 2) == 0, red, black).reshape(source.shape)]
    unnamed x1 -> x0, local copies, waits for them, and re-layouts: 4.84 us -> none
where the time goes in v7:
time: 146 us
  Pallas kernels  140 us (96%)
  other arithmetic  5.74 us (4%)
    pallas_call x1, Pallas kernels, local_solve(): pl.pallas_call(kernel, out_shape=[jax.ShapeDtypeStruct((pairs, rows, WIDT...  140 us
    select_n x1, other arithmetic, local_solve(): jnp.where(lax.rem(z + y + x, 2) == 0, red, black).reshape(source.shape)  5.1 us

profile of v7, /device:TPU:0, one launch (start us, length us, event | category | flops | bytes accessed | tf_op | source)
XLA Modules:
  0.0 145.9 jit_solution(7493106680421659308)
XLA Ops:
  0.0 0.6 fusion.1
  0.6 140.2 %multigrid.1 = (f32[48,96,128]{2,1,0:T(8,128)}, f32[48,96,128]{2,1,0:T(8,128)}) custom-call(f32[96,96,96]{2,1,0:T(8,128)} %f_hbm.1, f32[96,96,96]{2,1,0:T(8,128)} %u_hbm.1), custom_call_target="tpu_custom_call" | custom-call | tf_op jit(solution)/shard_map/multigrid/pallas_call | solution.py:685
  140.8 5.1 %broadcast_select_fusion = f32[48,2,96,96]{3,2,1,0:T(8,128)} fusion(f32[48,96,96]{2,1,0:T(8,128)} %bitcast.4, f32[48,96,96]{2,1,0:T(8,128)} %bitcast.3, pred[2,96,96]{2,1,0:T(8,128)(4,1)} %fusion.1), kind=kLoop, calls=%fused_computation | loop fusion | flops 884736 | bytes 7096320 | tf_op jit(solution)/shard_map/jit(_where)/select_n | solution.py:696

commit v8 on v6

--- a/solution.py
+++ b/solution.py
@@ -189,10 +189,6 @@
 
 
 def zero_start(u, hb, lv):
-    def clear(i):
-        u[1][i] = jnp.zeros(u[1].shape[1:], F32)
-    loop(u[1].shape[0], clear)
-
     def plane(k):
         u[0][lv.zs + k, lv.row, :] = lv.scaled(hb[0][lv.zs + k, lv.row, :])
     grouped(lv.planes, lv.unroll, plane)
@@ -527,6 +523,7 @@
                 device_id=peer, device_id_type=MESH)
             copy.start()
             copies.append(copy)
+        clear_all((u2b, u3b, u4b))
         for n in range(1, len(peers)):
             dz, dy = divmod(n, 2)
             copies[n].wait_recv()
@@ -596,6 +593,7 @@
         Columns(h1, l1, xs1, xr2.at[cycle], TILE).finish()
         faces = Faces(h1, l1, cycle)
         Columns(us[0], l0, xs, xr1.at[cycle], 4).finish()
+        clear_all((u1b,))
         faces.finish()
 
         @pl.when(cycle == 0)

time: 146 us -> 145 us (level)
  no operation moved by 1% of the time
where the time goes in v8:
time: 145 us
  Pallas kernels  140 us (97%)
  local copies, waits for them, and re-layouts  4.84 us (3%)
    pallas_call x1, Pallas kernels, local_solve(): pl.pallas_call(kernel, out_shape=jax.ShapeDtypeStruct(source.shape, F32),...  140 us
    unnamed x1, local copies, waits for them, and re-layouts  4.84 us

profile of v8, /device:TPU:0, one launch (start us, length us, event | category | flops | bytes accessed | tf_op | source)
XLA Modules:
  0.0 145.2 jit_solution(4642927467646113472)
XLA Ops:
  0.0 140.3 %multigrid.1 = f32[96,96,96]{2,1,0:T(8,128)} custom-call(f32[96,96,96]{2,1,0:T(8,128)} %f_hbm.1, f32[96,96,96]{2,1,0:T(8,128)} %u_hbm.1), custom_call_target="tpu_custom_call" | custom-call | tf_op jit(solution)/shard_map/multigrid/pallas_call | solution.py:693
  140.3 4.8 %copy.4 = f32[96,96,96]{2,1,0:T(8,128)} copy(f32[96,96,96]{2,1,0:T(8,128)} %multigrid.1) | data formatting | bytes 7077888
